TPU v7x, 32 devices: a whole 2x2x4 slice. The times are simulated.
32 devices in a mesh: dp: 4 (over x, core), tensor: 8 (over z, y).
Axes of the slice: x: 2, y: 2, z: 4, core: 2. Of those that a mesh axis runs over, the one named last changes fastest.
Arguments:
- tokens: bfloat16 [96, 8, 4096], P('dp'), may hold values from -6 to 6
- norm_gain: float32 [4096], replicated, may hold values from 0.1 to 1.9
- in_weight: bfloat16 [4096, 2, 4096], P(None, None, 'tensor'), may hold values from -0.09375 to 0.09375
- group_weight: bfloat16 [4096, 1024], P(None, 'tensor'), may hold values from -0.09375 to 0.09375
- step_weight: bfloat16 [4096, 64], P(None, 'tensor'), may hold values from -0.09375 to 0.09375
- value_kernel: bfloat16 [4, 4096], P(None, 'tensor'), may hold values from -3 to 3
- value_offset: bfloat16 [4096], P('tensor'), may hold values from -3 to 3
- group_kernel: bfloat16 [4, 1024], P(None, 'tensor'), may hold values from -3 to 3
- group_offset: bfloat16 [1024], P('tensor'), may hold values from -3 to 3
- step_bias: float32 [64], P('tensor'), may hold values from -4 to 1
- decay_rate: float32 [64], P('tensor'), may hold values from 0.05 to 2
- skip_gain: float32 [64], P('tensor'), may hold values from 0.5 to 2
- out_gain: float32 [4096], P('tensor'), may hold values from 0.1 to 1.9
- out_weight: bfloat16 [4096, 4096], P('tensor'), may hold values from -0.09375 to 0.09375
- scan_state: bfloat16 [96, 64, 64, 128], P('dp', 'tensor'), may hold values from -6 to 6
- value_cache: bfloat16 [96, 3, 4096], P('dp', None, 'tensor'), may hold values from -6 to 6
- group_cache: bfloat16 [96, 3, 1024], P('dp', None, 'tensor'), may hold values from -6 to 6
- accepted: int32 [96], P('dp'), may hold values from 0 to 8, as said below
- draft_lengths: int32 [96], P('dp'), may hold values from 1 to 8, as said below
- live_flags: int32 [96], P('dp'), may hold values 0 or 1
Outputs:
- layer_out: bfloat16 [96, 8, 4096], P('dp')
- kept_state: bfloat16 [96, 64, 64, 128], P('dp', 'tensor')
- value_kept: bfloat16 [96, 3, 4096], P('dp', None, 'tensor')
- group_kept: bfloat16 [96, 3, 1024], P('dp', None, 'tensor')
- accepted_total: int32 [1], replicated
Inputs may be any that keep to these rules, and one draw needn't show every extreme that they name: `draft_lengths`: positions at or after a request's draft length are padding. `accepted`: never more than the same request's draft length.
All inputs are finite; a program needn't handle non-finite values.
Results may differ from a plain program's by a relative error of at most 0.012.
Values may be sent and summed in bfloat16 or wider, within the bound.
A program may use at most 128 MiB of HBM per device.

v0:
```python
import jax
import jax.numpy as jnp
from jax import lax
from jax.experimental import pallas as pl
from jax.experimental.pallas import tpu as pltpu
from jax.sharding import PartitionSpec as P

EPSILON = 1e-05


def narrow(value):
    return value.astype(jnp.bfloat16)


def swapped(value, axis, distance):
    mask = 2**distance
    pairs = [(source, source ^ mask) for source in range(lax.axis_size(axis))]
    return lax.ppermute(value, axis, pairs)


def convolve(window, fresh_rows, kernel, offset):
    sequence = jnp.concatenate([window, fresh_rows], axis=1)
    length = fresh_rows.shape[1]
    summed = jnp.zeros(fresh_rows.shape, jnp.float32) + offset.astype(jnp.float32)
    for tap_index in range(kernel.shape[0]):
        summed = summed + kernel[tap_index].astype(jnp.float32) * sequence[
            :, tap_index : tap_index + length
        ].astype(jnp.float32)
    return (jax.nn.silu(summed), sequence)


def keep_window(sequence, kept_count, width_rows):
    kept = sequence[:, :width_rows]
    for start_row in range(1, sequence.shape[1] - width_rows + 1):
        chosen = (kept_count == start_row)[:, None, None]
        kept = jnp.where(chosen, sequence[:, start_row : start_row + width_rows], kept)
    return kept


MESH = pl.DeviceIdType.MESH


def project_kernel(
    normalized_ref,
    weight_ref,
    count_ref,
    out_ref,
    total_ref,
    weight_buf,
    pair_send,
    pair_recv,
    far_send,
    far_recv,
    kept_acc,
    count_recv,
    weight_sem,
    pair_sems,
    far_sems,
    pair_out_sems,
    far_out_sems,
    count_sems,
):
    members = lax.axis_size("tensor")
    fars = members // 2
    me = lax.axis_index("tensor")
    far, near = me // 2, me % 2
    partner = far * 2 + (1 - near)
    width = out_ref.shape[1] // members
    groups = lax.axis_size("dp")
    group = lax.axis_index("dp")
    parts, height = kept_acc.shape[:2]

    def far_at(step):
        return lax.rem(far + 1 + step, fars)

    def columns(block):
        return pl.ds(pl.multiple_of(block * width, width), width)

    order = [far_at(step) * 2 + (1 - near) for step in range(fars)]
    order += [far_at(step) * 2 + near for step in range(fars)]
    loads = [
        pltpu.make_async_copy(
            weight_ref.at[:, columns(block)], weight_buf.at[slot], weight_sem.at[slot]
        )
        for slot, block in enumerate(order)
    ]
    for load in loads:
        load.start()

    barrier = pltpu.get_barrier_semaphore()
    pl.semaphore_signal(barrier, inc=1, device_id={"tensor": partner}, device_id_type=MESH)
    for step in range(fars - 1):
        pl.semaphore_signal(
            barrier, inc=1, device_id={"tensor": far_at(step) * 2 + near}, device_id_type=MESH
        )
    for hop in range(groups - 1):
        pl.semaphore_signal(
            barrier,
            inc=1,
            device_id={"dp": lax.rem(group + 1 + hop, groups)},
            device_id_type=MESH,
        )
    pl.semaphore_wait(barrier, fars + groups - 1)

    def product(part, slot):
        if part == 0:
            loads[slot].wait()
        return jnp.dot(
            normalized_ref[part * height : (part + 1) * height],
            weight_buf[slot],
            preferred_element_type=jnp.float32,
        )

    def remote(source, target, sems, index, device):
        return pltpu.make_async_remote_copy(
            src_ref=source,
            dst_ref=target,
            send_sem=sems.at[0, index],
            recv_sem=sems.at[1, index],
            device_id={"tensor": device},
            device_id_type=MESH,
        )

    count_copies = []
    for hop in range(groups - 1):
        copy = pltpu.make_async_remote_copy(
            src_ref=count_ref,
            dst_ref=count_recv.at[hop],
            send_sem=count_sems.at[0, hop],
            recv_sem=count_sems.at[1, hop],
            device_id={"dp": lax.rem(group + 1 + hop, groups)},
            device_id_type=MESH,
        )
        copy.start()
        count_copies.append(copy)

    pair_copies, far_copies, pair_outs, far_outs = [], [], [], []
    for part in range(parts):
        for step in range(fars):
            slot = part * fars + step
            pair_send[slot] = product(part, step).astype(pair_send.dtype)
            copy = remote(pair_send.at[slot], pair_recv.at[slot], pair_sems, slot, partner)
            copy.start()
            pair_copies.append(copy)
    for part in range(parts):
        for step in range(fars):
            summed = product(part, fars + step)
            pair_copies[part * fars + step].wait_recv()
            summed = summed + pair_recv[part * fars + step].astype(jnp.float32)
            if step < fars - 1:
                slot = part * (fars - 1) + step
                far_send[slot] = summed.astype(far_send.dtype)
                copy = remote(
                    far_send.at[slot],
                    far_recv.at[slot],
                    far_sems,
                    slot,
                    far_at(step) * 2 + near,
                )
                copy.start()
                far_copies.append(copy)
            else:
                kept_acc[part] = summed
    for part in range(parts):
        rows = pl.ds(part * height, height)
        total = kept_acc[part]
        for step in range(fars - 1):
            slot = part * (fars - 1) + step
            far_copies[slot].wait_recv()
            total = total + far_recv[slot].astype(jnp.float32)
        mine = out_ref.at[rows, columns(me)]
        out_ref[rows, columns(me)] = total.astype(out_ref.dtype)
        copy = remote(mine, mine, pair_out_sems, part * fars, partner)
        copy.start()
        pair_outs.append(copy)
        for step in range(fars - 1):
            slot = part * (fars - 1) + step
            copy = remote(mine, mine, far_out_sems, slot, far_at(step) * 2 + near)
            copy.start()
            far_outs.append(copy)
    for part in range(parts):
        rows = pl.ds(part * height, height)
        for step in range(fars - 1):
            far_outs[part * (fars - 1) + step].wait_recv()
            source = lax.rem(far - 1 - step + 2 * fars, fars) * 2 + near
            there = out_ref.at[rows, columns(source)]
            copy = remote(there, there, pair_out_sems, part * fars + step + 1, partner)
            copy.start()
            pair_outs.append(copy)
    count = count_ref[...]
    for hop in range(groups - 1):
        count_copies[hop].wait_recv()
        count = count + count_recv[hop]
    total_ref[...] = count
    for copy in pair_outs:
        copy.wait_recv()
    for copy in pair_copies + far_copies + far_outs + pair_outs + count_copies:
        copy.wait_send()


def project(normalized, out_weight, own_total):
    rows, inner = normalized.shape
    model_width = out_weight.shape[1]
    members = lax.axis_size("tensor")
    groups = lax.axis_size("dp")
    fars = members // 2
    parts = 2 if rows % 32 == 0 else 1
    width = model_width // members
    block = (rows // parts, width)
    return pl.pallas_call(
        project_kernel,
        out_shape=[
            jax.ShapeDtypeStruct((rows, model_width), jnp.bfloat16),
            jax.ShapeDtypeStruct(own_total.shape, jnp.int32),
        ],
        in_specs=[
            pl.BlockSpec(memory_space=pltpu.VMEM),
            pl.BlockSpec(memory_space=pl.ANY),
            pl.BlockSpec(memory_space=pltpu.VMEM),
        ],
        out_specs=[pl.BlockSpec(memory_space=pltpu.VMEM)] * 2,
        scratch_shapes=[
            pltpu.VMEM((members, inner, width), jnp.bfloat16),
            pltpu.VMEM((parts * fars, *block), jnp.bfloat16),
            pltpu.VMEM((parts * fars, *block), jnp.bfloat16),
            pltpu.VMEM((parts * (fars - 1), *block), jnp.bfloat16),
            pltpu.VMEM((parts * (fars - 1), *block), jnp.bfloat16),
            pltpu.VMEM((parts, *block), jnp.float32),
            pltpu.VMEM((groups - 1, *own_total.shape), jnp.int32),
            pltpu.SemaphoreType.DMA((members,)),
            pltpu.SemaphoreType.DMA((2, parts * fars)),
            pltpu.SemaphoreType.DMA((2, parts * (fars - 1))),
            pltpu.SemaphoreType.DMA((2, parts * fars)),
            pltpu.SemaphoreType.DMA((2, parts * (fars - 1))),
            pltpu.SemaphoreType.DMA((2, groups - 1)),
        ],
        compiler_params=pltpu.CompilerParams(
            collective_id=0, has_side_effects=True, vmem_limit_bytes=40 * 1024 * 1024
        ),
    )(normalized, out_weight, own_total)


def local(
    tokens,
    norm_gain,
    in_weight,
    group_weight,
    step_weight,
    value_kernel,
    value_offset,
    group_kernel,
    group_offset,
    step_bias,
    decay_rate,
    skip_gain,
    out_gain,
    out_weight,
    scan_state,
    value_cache,
    group_cache,
    accepted,
    draft_lengths,
    live_flags,
):
    requests, positions, model_width = tokens.shape
    row_total = requests * positions
    head_count = step_bias.shape[0]
    inner_dev = value_offset.shape[0]
    head_dim = inner_dev // head_count
    tap_count = value_kernel.shape[0]
    kept_count = accepted * live_flags
    wide = tokens.astype(jnp.float32)
    normed = (
        (wide * lax.rsqrt(jnp.mean(wide * wide, axis=2, keepdims=True) + EPSILON) * norm_gain)
        .astype(jnp.bfloat16)
        .reshape(row_total, model_width)
    )
    parity = lax.axis_index("tensor") % 2
    inner_sum = jnp.einsum("rd,dgi->rgi", normed, in_weight, preferred_element_type=jnp.float32)
    group_sum = jnp.dot(normed, group_weight, preferred_element_type=jnp.float32)
    step_raw = jnp.dot(normed, step_weight, preferred_element_type=jnp.float32)
    inner_proj = inner_sum.astype(jnp.bfloat16).reshape(requests, positions, 2 * inner_dev)
    gate_part = inner_proj[:, :, :inner_dev]
    value_part = inner_proj[:, :, inner_dev:]
    group_proj = group_sum.astype(jnp.bfloat16).reshape(requests, positions, group_weight.shape[1])
    value_conv, value_seq = convolve(value_cache, value_part, value_kernel, value_offset)
    own_conv, group_seq = convolve(group_cache, group_proj, group_kernel, group_offset)
    other_conv = swapped(own_conv, "tensor", 0)
    input_map = jnp.where(parity == 0, own_conv, other_conv)
    output_map = jnp.where(parity == 0, other_conv, own_conv)
    values = value_conv.reshape(requests, positions, head_count, head_dim)
    step_size = jax.nn.softplus(step_raw.reshape(requests, positions, head_count) + step_bias)
    log_decay = -step_size * decay_rate
    prefix = jnp.concatenate(
        [jnp.zeros((requests, 1, head_count), jnp.float32), jnp.cumsum(log_decay, axis=1)], axis=1
    )
    after_step = prefix[:, 1:]
    alignment = jnp.einsum("rsn,rjn->rsj", narrow(output_map), narrow(input_map), preferred_element_type=jnp.float32)
    causal = (jnp.arange(positions)[:, None] >= jnp.arange(positions)[None, :])[None, :, :, None]
    spread = after_step[:, :, None, :] - after_step[:, None, :, :]
    weights_mix = (
        jnp.where(causal, jnp.exp(jnp.where(causal, spread, 0.0)), 0.0)
        * step_size[:, None, :, :]
        * alignment[:, :, :, None]
    )
    within = jnp.einsum("rsjh,rjhp->rshp", narrow(weights_mix), narrow(values), preferred_element_type=jnp.float32)
    initial = scan_state.astype(jnp.float32)
    carried = (
        jnp.einsum("rhpn,rsn->rshp", scan_state, narrow(output_map), preferred_element_type=jnp.float32)
        * jnp.exp(after_step)[:, :, :, None]
    )
    head_out = within + carried + skip_gain[:, None] * values
    one_hot = (jnp.arange(positions + 1)[None, :] == kept_count[:, None]).astype(jnp.float32)
    prefix_kept = jnp.sum(one_hot[:, :, None] * prefix, axis=1)
    before_kept = (jnp.arange(positions)[None, :] < kept_count[:, None])[:, :, None]
    keep_weight = (
        jnp.where(
            before_kept,
            jnp.exp(jnp.where(before_kept, prefix_kept[:, None, :] - after_step, 0.0)),
            0.0,
        )
        * step_size
    )
    weighted = keep_weight[:, :, :, None] * values
    kept_state = (
        jnp.exp(prefix_kept)[:, :, None, None] * initial
        + jnp.einsum("rjhp,rjn->rhpn", narrow(weighted), narrow(input_map), preferred_element_type=jnp.float32)
    ).astype(jnp.bfloat16)
    gated = head_out.reshape(requests, positions, inner_dev) * jax.nn.silu(
        gate_part.astype(jnp.float32)
    )
    own_squares = jnp.sum(gated * gated, axis=2)
    other_squares = swapped(own_squares, "tensor", 0)
    scale_rows = lax.rsqrt((own_squares + other_squares) / (2 * inner_dev) + EPSILON)
    valid_rows = (jnp.arange(positions)[None, :] < draft_lengths[:, None]) & (
        live_flags[:, None] == 1
    )
    normalized = (
        jnp.where(valid_rows[:, :, None], gated * scale_rows[:, :, None] * out_gain, 0.0)
        .astype(jnp.bfloat16)
        .reshape(row_total, inner_dev)
    )
    own_total = jnp.broadcast_to(jnp.sum(kept_count), (8, 128))
    layer_rows, totals = project(normalized, out_weight, own_total)
    accepted_total = totals[0, :1]
    value_kept = keep_window(value_seq, kept_count, tap_count - 1)
    group_kept = keep_window(group_seq, kept_count, tap_count - 1)
    return (
        layer_rows.reshape(requests, positions, model_width),
        kept_state,
        value_kept,
        group_kept,
        accepted_total,
    )


def solution(mesh):
    placed = (
        P("dp", None, None),
        P(),
        P(None, None, "tensor"),
        P(None, "tensor"),
        P(None, "tensor"),
        P(None, "tensor"),
        P("tensor"),
        P(None, "tensor"),
        P("tensor"),
        P("tensor"),
        P("tensor"),
        P("tensor"),
        P("tensor"),
        P("tensor", None),
        P("dp", "tensor", None, None),
        P("dp", None, "tensor"),
        P("dp", None, "tensor"),
        P("dp"),
        P("dp"),
        P("dp"),
    )
    return jax.shard_map(
        local,
        mesh=mesh,
        in_specs=placed,
        out_specs=(
            P("dp", None, None),
            P("dp", "tensor", None, None),
            P("dp", None, "tensor"),
            P("dp", None, "tensor"),
            P(),
        ),
        check_vma=False,
    )
```

profile of v0, /device:TPU:0, one launch (start us, length us, event | category | flops | bytes accessed | tf_op | source)
XLA Modules:
  0.0 92.5 jit_solution(3550883104792727496)
XLA Ops:
  0.7 0.8 convert_element_type.175
  1.5 0.8 bitcast_convert_fusion.3
  2.4 1.8 %fusion.2 = f32[24,8]{1,0:T(8,128)S(1)} fusion(bf16[24,8,4096]{2,1,0:T(8,128)(2,1)} %param.20), kind=kLoop, calls=%fused_computation.5 | loop fusion | flops 2359104 | bytes 1573632 | tf_op jit(solution)/shard_map/reduce_sum | solution.py:274
  4.2 0.7 constant_dynamic-update-slice_fusion.1
  4.9 2.1 %fusion.18 = bf16[24,8,128]{2,1,0:T(8,128)(2,1)S(1)} fusion(bf16[4096,128]{1,0:T(8,128)(2,1)S(1)} %copy-done, bf16[24,8,4096]{2,1,0:T(8,128)(2,1)} %param.20, f32[4096]{0:T(1024)} %param.21, f32[24,8]{1,0:T(8,128)S(1)} %add_rsqrt_fusion.1), kind=kOutput, calls=%fused_computation.18 | convolution fusion | flops 204496896 | bytes 2687744 | tf_op jit(solution)/shard_map/dot_general | solution.py:280
  7.1 3.1 %collective-permute-start = (bf16[24,8,128]{2,0,1:T(8,128)(2,1)S(1)}, bf16[24,8,128]{2,0,1:T(8,128)(2,1)}, u32[]{:S(2)}, u32[]{:S(2)}) collective-permute-start(bf16[24,8,128]{2,0,1:T(8,128)(2,1)S(1)} %divide_multiply_fusion.1), channel_id=1, source_target_pairs={{0,1},{1,0},{2,3},{3,2},{4,5},{5,4},{6,7},{7,6},{8,9},{9,8},{10,11... | collective-permute-start | bytes 147464 | tf_op jit(solution)/shard_map/ppermute | solution.py:18
  10.9 5.2 %fusion.10 = bf16[192,2,512]{2,0,1:T(8,128)(2,1)S(1)} fusion(bf16[4096,2,512]{2,1,0:T(2,128)(2,1)} %param.22, bf16[24,8,4096]{2,1,0:T(8,128)(2,1)S(1)} %copy-done.2, f32[4096]{0:T(1024)S(1)} %copy-done.16, f32[24,8]{1,0:T(8,128)S(1)} %add_rsqrt_fusion.1), kind=kOutput, calls=%fused_computation.15 | convolution fusion | flops 1613955072 | bytes 10371840 | tf_op jit(solution)/shard_map/rd,dgi->rgi/dot_general | solution.py:279
  16.9 0.7 fusion.64
  17.6 0.6 fusion.47
  18.7 0.7 fusion.65
  19.4 2.1 %negate_multiply_fusion = (f32[24,8,8]{2,1,0:T(8,128)S(1)}, f32[24,8,8]{2,1,0:T(8,128)S(1)}) fusion(f32[8]{0:T(128)S(1)} %copy-done.17, f32[8]{0:T(128)S(1)} %copy-done.18, bf16[4096,8]{0,1:T(8,128)(2,1)S(1)} %copy-done.15, bf16[24,8,4096]{2,1,0:T(8,128)(2,1)} %param.20, f32[4096]{0:T(1024)S(1)} %copy-done.16, f32[24,8]{1,0:T(8,128)S(1)} %add_rsqrt_fusion.1), kind=kOutput, calls=%fused_computation.67 | convolution fusion | flops 15742464 | bytes 1667904 | tf_op jit(solution)/shard_map/dot_general | solution.py:281
  21.8 0.5 copy-done.3
  22.6 0.6 iota_compare_fusion.3
  23.2 1.3 %reduce_sum.38 = s32[]{:T(128)} reduce(s32[24]{0:T(128)} %copy-done.9, s32[]{:T(128)} %constant.25.clone.1), dimensions={0}, to_apply=%region_3.4 | reduce | flops 23 | bytes 104 | tf_op jit(solution)/shard_map/reduce_sum | solution.py:343
  24.5 1.3 %exp.41 = f32[24,8]{1,0:T(8,128)} exponential(f32[24,8]{1,0:T(8,128)} %copy-done.3) | non-fusion elementwise | bytes 1536 | tf_op jit(solution)/shard_map/exp | solution.py:326
  26.1 0.7 copy.65
  26.8 0.8 select_convert_fusion.1
  27.7 4.4 %convolution_multiply_fusion = f32[24,8,8,64]{3,1,2,0:T(8,128)S(1)} fusion(bf16[24,8,64,128]{3,2,1,0:T(8,128)(2,1)} %param.34, f32[24,8,8]{1,2,0:T(8,128)S(1)} %copy.53, bf16[24,8,128]{2,0,1:T(8,128)(2,1)S(1)} %get-tuple-element.21), kind=kOutput, calls=%fused_computation.14 | convolution fusion | flops 25264128 | bytes 3594240 | tf_op jit(solution)/shard_map/rhpn,rsn->rshp/dot_general | solution.py:309
  32.2 0.5 fusion.9
  33.4 5.4 %add_convert_fusion = bf16[24,8,64,128]{3,2,1,0:T(8,128)(2,1)} fusion(bf16[24,8,64,128]{3,2,1,0:T(8,128)(2,1)} %param.34, f32[24,8]{1,0:T(8,128)S(1)} %copy-done.6, bf16[24,8,8,64]{3,2,1,0:T(8,128)(2,1)S(1)} %get-tuple-element.16, bf16[24,8,128]{2,0,1:T(8,128)(2,1)S(1)} %get-tuple-element.20), kind=kOutput, calls=%fused_computation.2 | convolution fusion | flops 31457280 | bytes 6537984 | tf_op jit(solution)/shard_map/rjhp,rjn->rhpn/dot_general | solution.py:327
  39.1 0.6 broadcast_in_dim.191.count_ref
  39.8 51.1 %shard_map.227 = (bf16[192,4096]{1,0:T(8,128)(2,1)S(1)}, s32[8,128]{1,0:T(8,128)S(1)}) custom-call(bf16[192,512]{1,0:T(8,128)(2,1)S(1)} %fusion.36.normalized_ref, bf16[512,4096]{1,0:T(8,128)(2,1)S(1)} %copy-done.1, s32[8,128]{1,0:T(8,128)S(1)} %broadcast_in_dim.191.count_ref), custom_call_target="tpu_custom_call" | custom-call | tf_op jit(solution)/shard_map/pallas_call | solution.py:210
  90.9 0.5 slice.137
  91.4 1.1 %copy.96 = bf16[24,8,4096]{2,1,0:T(8,128)(2,1)} copy(bf16[24,8,4096]{2,1,0:T(8,128)(2,1)S(1)} %bitcast.60) | data formatting | bytes 3145728
  (72 shorter events, 4.0 us)
Async XLA Ops:
  0.6 4.3 %copy-start = (bf16[4096,128]{1,0:T(8,128)(2,1)S(1)}, bf16[4096,128]{1,0:T(8,128)(2,1)}, u32[]{:S(2)}) copy-start(bf16[4096,128]{1,0:T(8,128)(2,1)} %param.23) | copy-start | bytes 3145732
  0.6 10.2 %copy-start.2 = (bf16[24,8,4096]{2,1,0:T(8,128)(2,1)S(1)}, bf16[24,8,4096]{2,1,0:T(8,128)(2,1)}, u32[]{:S(2)}) copy-start(bf16[24,8,4096]{2,1,0:T(8,128)(2,1)} %param.20) | copy-start | bytes 4718596
  0.7 10.2 %copy-start.16 = (f32[4096]{0:T(1024)S(1)}, f32[4096]{0:T(1024)}, u32[]{:S(2)}) copy-start(f32[4096]{0:T(1024)} %param.21) | copy-start | bytes 49156
  0.7 9.5 %copy-start.13 = (s32[24]{0:T(128)S(1)}, s32[24]{0:T(128)}, u32[]{:S(2)}) copy-start(s32[24]{0:T(128)} %param.39) | copy-start | bytes 292
  0.7 9.5 %copy-start.12 = (s32[24]{0:T(128)S(1)}, s32[24]{0:T(128)}, u32[]{:S(2)}) copy-start(s32[24]{0:T(128)} %param.37) | copy-start | bytes 292
  0.7 10.1 %copy-start.11 = (bf16[512]{0:T(512)(128)(2,1)S(1)}, bf16[512]{0:T(512)(128)(2,1)}, u32[]{:S(2)}) copy-start(bf16[512]{0:T(512)(128)(2,1)} %param.26) | copy-start | bytes 3076
  0.7 10.1 %copy-start.7 = (bf16[4,512]{1,0:T(4,128)(2,1)S(1)}, bf16[4,512]{1,0:T(4,128)(2,1)}, u32[]{:S(2)}) copy-start(bf16[4,512]{1,0:T(4,128)(2,1)} %param.25) | copy-start | bytes 12292
  0.7 10.1 %copy-start.5 = (bf16[24,3,512]{2,0,1:T(8,128)(2,1)S(1)}, bf16[24,3,512]{2,0,1:T(8,128)(2,1)}, u32[]{:S(2)}) copy-start(bf16[24,3,512]{2,0,1:T(8,128)(2,1)} %param.35) | copy-start | bytes 221188
  7.1 19.7 %collective-permute-start = (bf16[24,8,128]{2,0,1:T(8,128)(2,1)S(1)}, bf16[24,8,128]{2,0,1:T(8,128)(2,1)}, u32[]{:S(2)}, u32[]{:S(2)}) collective-permute-start(bf16[24,8,128]{2,0,1:T(8,128)(2,1)S(1)} %divide_multiply_fusion.1), channel_id=1, source_target_pairs={{0,1},{1,0},{2,3},{3,2},{4,5},{5,4},{6,7},{7,6},{8,9},{9,8},{10,11... | collective-permute-start | bytes 147464 | tf_op jit(solution)/shard_map/ppermute | solution.py:18
  10.2 0.5 copy-start.9
  10.9 6.0 %copy-start.4 = (bf16[24,3,128]{2,0,1:T(8,128)(2,1)S(1)}, bf16[24,3,128]{2,0,1:T(8,128)(2,1)}, u32[]{:S(2)}) copy-start(bf16[24,3,128]{2,0,1:T(8,128)(2,1)} %param.36) | copy-start | bytes 55300
  16.1 2.6 %copy-start.14 = (s32[24]{0:T(128)S(1)}, s32[24]{0:T(128)}, u32[]{:S(2)}) copy-start(s32[24]{0:T(128)} %param.38) | copy-start | bytes 292
  16.1 3.3 %copy-start.15 = (bf16[4096,8]{0,1:T(8,128)(2,1)S(1)}, bf16[4096,8]{0,1:T(8,128)(2,1)}, u32[]{:S(2)}) copy-start(bf16[4096,8]{0,1:T(8,128)(2,1)} %param.24) | copy-start | bytes 196612
  16.1 3.3 %copy-start.17 = (f32[8]{0:T(128)S(1)}, f32[8]{0:T(128)}, u32[]{:S(2)}) copy-start(f32[8]{0:T(128)} %param.30) | copy-start | bytes 100
  16.2 3.2 %copy-start.18 = (f32[8]{0:T(128)S(1)}, f32[8]{0:T(128)}, u32[]{:S(2)}) copy-start(f32[8]{0:T(128)} %param.29) | copy-start | bytes 100
  21.7 0.6 copy-start.3
  26.1 6.1 %copy-start.19 = (f32[8]{0:T(128)S(1)}, f32[8]{0:T(128)}, u32[]{:S(2)}) copy-start(f32[8]{0:T(128)} %param.31) | copy-start | bytes 100
  26.1 6.0 %copy-start.20 = (pred[8,8]{1,0:T(8,128)(4,1)S(1)}, pred[8,8]{1,0:T(8,128)(4,1)}, u32[]{:S(2)}) copy-start(pred[8,8]{1,0:T(8,128)(4,1)} %iota_compare_fusion.3) | copy-start | bytes 196
  32.2 1.2 %copy-start.6 = (f32[24,8]{1,0:T(8,128)S(1)}, f32[24,8]{1,0:T(8,128)}, u32[]{:S(2)}) copy-start(f32[24,8]{1,0:T(8,128)} %exp.41) | copy-start | bytes 2308
  33.3 5.6 %collective-permute-start.1 = (f32[24,8]{1,0:T(8,128)S(1)}, f32[24,8]{1,0:T(8,128)S(1)}, u32[]{:S(2)}, u32[]{:S(2)}) collective-permute-start(f32[24,8]{1,0:T(8,128)S(1)} %multiply_reduce_fusion), channel_id=1, source_target_pairs={{0,1},{1,0},{2,3},{3,2},{4,5},{5,4},{6,7},{7,6},{8,9},{9,8},{10,11... | collective-permute-start | bytes 2312 | tf_op jit(solution)/shard_map/ppermute | solution.py:18
  33.4 5.5 %copy-start.8 = (pred[24,8]{1,0:T(8,128)(4,1)S(1)}, pred[24,8]{1,0:T(8,128)(4,1)}, u32[]{:S(2)}) copy-start(pred[24,8]{1,0:T(8,128)(4,1)} %fusion.65) | copy-start | bytes 580
  33.4 5.5 %copy-start.10 = (f32[512]{0:T(512)S(1)}, f32[512]{0:T(512)}, u32[]{:S(2)}) copy-start(f32[512]{0:T(512)} %param.32) | copy-start | bytes 6148
  33.4 6.3 %copy-start.1 = (bf16[512,4096]{1,0:T(8,128)(2,1)S(1)}, bf16[512,4096]{1,0:T(8,128)(2,1)}, u32[]{:S(2)}) copy-start(bf16[512,4096]{1,0:T(8,128)(2,1)} %weight_ref.1) | copy-start | bytes 12582916
where the time goes:
time: 93 us; the launch traced here: 92.5 us
  Pallas kernels  51.1 us (55%)
  matrix products  19.9 us (21%)
  other arithmetic  9.74 us (10%)
  local copies, waits for them, and re-layouts  7.55 us (8%)
  starting transfers between devices  3.14 us (3%)
  between operations  1.06 us (1%)
    pallas_call x1, Pallas kernels, project(): pl.pallas_call(project_kernel, out_shape=[jax.ShapeDtypeStruct((rows, mod...  51.1 us
    dot_general x1, matrix products, local(): jnp.einsum('rjhp,rjn->rhpn', narrow(weighted), narrow(input_map), preferr...  5.44 us
    dot_general x1, matrix products, local(): jnp.einsum('rd,dgi->rgi', normed, in_weight, preferred_element_type=jnp.f...  5.24 us
    dot_general x1, matrix products, local(): jnp.einsum('rhpn,rsn->rshp', scan_state, narrow(output_map), preferred_el...  4.42 us
    unnamed x46, local copies, waits for them, and re-layouts  3.61 us
    ppermute x2, starting transfers between devices, swapped(): return lax.ppermute(value, axis, pairs)  3.14 us
    dot_general x1, matrix products, local(): jnp.dot(normed, group_weight, preferred_element_type=jnp.float32)  2.08 us
    dot_general x1, matrix products, local(): step_raw = jnp.dot(normed, step_weight, preferred_element_type=jnp.float32)  2.06 us
  transfers between devices with their start and end apart: 2, of which 0 were waited for; matrix products, arithmetic and copies ran while one was open for 23% of the time, Pallas kernels for 0%

commit v1 on v0

v1 whole, which is shorter than its diff:
```python
import jax
import jax.numpy as jnp
from jax import lax
from jax.experimental import pallas as pl
from jax.experimental.pallas import tpu as pltpu
from jax.sharding import PartitionSpec as P

EPSILON = 1e-05
MESH = pl.DeviceIdType.MESH
F32 = jnp.float32
BF16 = jnp.bfloat16


def iota(shape, axis):
    return lax.broadcasted_iota(jnp.int32, shape, axis)


def dot(a, b):
    return jnp.dot(a, b, preferred_element_type=F32)


def dot_nt(a, b):
    return lax.dot_general(a, b, (((1,), (1,)), ((), ())), preferred_element_type=F32)


def dot_tn(a, b):
    return lax.dot_general(a, b, (((0,), (0,)), ((), ())), preferred_element_type=F32)


def dot_split(a, b):
    high = a.astype(BF16)
    low = (a - high.astype(F32)).astype(BF16)
    return dot(high, b) + dot(low, b)


def silu(v):
    return v * (1.0 / (1.0 + jnp.exp(-v)))


def spread_cache(cache, rows, positions, first):
    depth, requests, width = cache.shape
    flat = cache.reshape(depth * requests, width)
    row = iota((rows, depth * requests), 0)
    col = iota((rows, depth * requests), 1)
    place = row % positions - (positions - depth)
    chosen = (col == place * requests + first + row // positions) & (place >= 0)
    return dot(chosen.astype(BF16), flat)


def convolve(fresh, cached, kernel, offset, positions):
    rows, width = fresh.shape
    taps = kernel.shape[0]
    fresh = fresh.reshape(rows // positions, positions, width)
    cached = cached.reshape(rows // positions, positions, width)
    place = iota(fresh.shape, 1)
    total = offset[None] + kernel[taps - 1 : taps][None] * fresh
    for shift in range(1, taps):
        merged = jnp.where(place < positions - shift, fresh, cached)
        moved = pltpu.roll(merged, shift, axis=1)
        total = total + kernel[taps - 1 - shift : taps - shift][None] * moved
    return silu(total).reshape(rows, width)


def prepare_kernel(
    accepted_hbm,
    draft_hbm,
    live_hbm,
    tokens_hbm,
    gain_hbm,
    weight_hbm,
    step_weight_hbm,
    cache_hbm,
    kernel_hbm,
    offset_hbm,
    bias_hbm,
    rate_hbm,
    normed_ref,
    conv_ref,
    mix_ref,
    keep_ref,
    after_ref,
    scale_ref,
    valid_ref,
    fresh_pick_ref,
    cache_pick_ref,
    group_kept_hbm,
    total_ref,
    accepted_ref,
    draft_ref,
    live_ref,
    tokens_ref,
    gain_ref,
    weight_ref,
    step_weight_ref,
    cache_ref,
    kernel_ref,
    offset_ref,
    bias_ref,
    rate_ref,
    group_kept_ref,
    load_sems,
    kept_sem,
):
    sources = (gain_hbm, tokens_hbm, weight_hbm, step_weight_hbm, cache_hbm)
    sources += (kernel_hbm, offset_hbm, bias_hbm, rate_hbm, accepted_hbm, draft_hbm, live_hbm)
    targets = (gain_ref, tokens_ref, weight_ref, step_weight_ref, cache_ref)
    targets += (kernel_ref, offset_ref, bias_ref, rate_ref, accepted_ref, draft_ref, live_ref)
    loads = [
        pltpu.make_async_copy(source, target, load_sems.at[index])
        for index, (source, target) in enumerate(zip(sources, targets))
    ]
    for load in loads:
        load.start()
    rows, model_width = tokens_ref.shape
    requests = accepted_ref.shape[0]
    positions = rows // requests
    heads = bias_ref.shape[1]
    depth = cache_ref.shape[0]
    lanes = positions * heads
    step = 16 if rows % 16 == 0 else 8
    loads[0].wait()
    loads[1].wait()
    for start in range(0, rows, step):
        wide = tokens_ref[start : start + step].astype(F32)
        mean = jnp.sum(wide * wide, axis=1, keepdims=True) / model_width
        normed_ref[start : start + step] = (
            wide * lax.rsqrt(mean + EPSILON) * gain_ref[...]
        ).astype(BF16)
    for load in loads[2:]:
        load.wait()
    normed = normed_ref[...]
    group_proj = dot(normed, weight_ref[...]).astype(BF16)
    step_raw = dot_nt(normed, step_weight_ref[...])

    cache = cache_ref[...]
    cached = spread_cache(cache, rows, positions, 0)
    conv = convolve(
        group_proj.astype(F32),
        cached,
        kernel_ref[...].astype(F32),
        offset_ref[...].astype(F32),
        positions,
    )
    conv_ref[...] = conv.astype(BF16)

    counts = [accepted_ref[r] * live_ref[r] for r in range(requests)]
    total = counts[0]
    for count in counts[1:]:
        total = total + count
    total_ref[...] = jnp.full(total_ref.shape, total, jnp.int32)

    bias = jnp.concatenate([bias_ref[...]] * positions, axis=1)[None]
    rate = jnp.concatenate([rate_ref[...]] * positions, axis=1)[None]
    raw = jnp.concatenate([step_raw] * positions, axis=1).reshape(requests, positions, lanes)
    raw = raw + bias
    size = jnp.maximum(raw, 0.0) + jnp.log1p(jnp.exp(-jnp.abs(raw)))
    log_decay = -size * rate
    place = iota((requests, positions, lanes), 1)
    source = iota((requests, positions, lanes), 2) // heads
    after = log_decay
    shift = 1
    while shift < positions:
        after = after + jnp.where(place >= shift, pltpu.roll(after, shift, axis=1), 0.0)
        shift *= 2
    kept = jnp.stack([jnp.full((positions, lanes), count, jnp.int32) for count in counts])
    own = place == source
    after_source = jnp.sum(jnp.where(own, after, 0.0), axis=1, keepdims=True)
    size_source = jnp.sum(jnp.where(own, size, 0.0), axis=1, keepdims=True)
    causal = place >= source
    mix = jnp.where(causal, jnp.exp(jnp.where(causal, after - after_source, 0.0)), 0.0) * size_source
    kept_after = jnp.sum(jnp.where(place == kept - 1, after, 0.0), axis=1, keepdims=True)
    before = place < kept
    keep = jnp.where(before, jnp.exp(jnp.where(before, kept_after - after, 0.0)), 0.0) * size
    mix_ref[...] = mix.reshape(rows, lanes)
    keep_ref[...] = keep.reshape(rows, lanes)
    after_ref[...] = jnp.exp(after).reshape(rows, lanes)
    scale_ref[...] = jnp.exp(kept_after[:, 0, :heads])

    wide_lanes = valid_ref.shape[1]
    drafted = jnp.stack(
        [
            jnp.full((positions, wide_lanes), draft_ref[r] * (live_ref[r] == 1).astype(jnp.int32), jnp.int32)
            for r in range(requests)
        ]
    )
    valid = iota(drafted.shape, 1) < drafted
    valid_ref[...] = valid.astype(F32).reshape(rows, wide_lanes)

    def picks(width, position_of, request_of):
        shape = (requests, width)
        row = iota(shape, 0)
        count = jnp.zeros(shape, jnp.int32)
        for r in range(requests):
            count = jnp.where(row == r, counts[r], count)
        col = iota(shape, 1)
        return jnp.concatenate(
            [
                ((position_of(col) == count + t) & (request_of(col) == row)).astype(F32)
                for t in range(depth)
            ],
            axis=0,
        ).astype(BF16)

    fresh_pick = picks(rows, lambda col: col % positions + depth, lambda col: col // positions)
    cache_pick = picks(depth * requests, lambda col: col // requests, lambda col: col % requests)
    fresh_pick_ref[...] = fresh_pick
    cache_pick_ref[...] = cache_pick
    kept_rows = dot(fresh_pick, group_proj) + dot(cache_pick, cache.reshape(depth * requests, -1))
    group_kept_ref[...] = kept_rows.reshape(group_kept_ref.shape).astype(BF16)
    kept_copy = pltpu.make_async_copy(group_kept_ref, group_kept_hbm, kept_sem)
    kept_copy.start()
    kept_copy.wait()


def layer_kernel(
    scale_ref,
    skip_ref,
    inner_ref,
    conv_ref,
    mix_ref,
    keep_ref,
    after_ref,
    valid_ref,
    cache_ref,
    kernel_ref,
    offset_ref,
    gain_ref,
    count_ref,
    weight_hbm,
    state_hbm,
    out_buf,
    kept_buf,
    total_ref,
    weight_buf,
    state_buf,
    y_send,
    y_recv,
    z_send,
    z_recv,
    acc_buf,
    place_buf,
    map_recv,
    input_map,
    output_map,
    weighted_buf,
    sq_send,
    sq_recv,
    count_recv,
    weight_sem,
    state_sem,
    map_sems,
    sq_sems,
    y_sems,
    z_sems,
    o_sems,
    p_sems,
    count_sems,
):
    chunks, height, half = y_send.shape
    rows, inner = inner_ref.shape[1:]
    requests = state_buf.shape[0]
    positions = rows // requests
    lanes = mix_ref.shape[1]
    heads = lanes // positions
    head_dim = inner // heads
    per_chunk = requests // chunks
    depth = cache_ref.shape[0]

    members = lax.axis_size("tensor")
    fars = members // 2
    width = half // fars
    me = lax.axis_index("tensor")
    far, near = me // 2, me % 2
    partner = far * 2 + (1 - near)

    def far_at(step):
        return lax.rem(far + 1 + step, fars)

    def far_of(step):
        return lax.rem(far - 1 - step + 2 * fars, fars)

    groups = lax.axis_size("dp")
    group = lax.axis_index("dp")

    def cols(start, width):
        return pl.ds(pl.multiple_of(start, width), width)

    weight_loads = [
        pltpu.make_async_copy(
            weight_hbm.at[:, cols(block * half, half)],
            weight_buf.at[slot],
            weight_sem.at[slot],
        )
        for slot, block in enumerate((1 - near, near))
    ]
    state_loads = [
        pltpu.make_async_copy(
            state_hbm.at[pl.ds(c * per_chunk, per_chunk)],
            state_buf.at[pl.ds(c * per_chunk, per_chunk)],
            state_sem.at[c],
        )
        for c in range(chunks)
    ]
    state_loads[0].start()
    weight_loads[0].start()
    weight_loads[1].start()
    for load in state_loads[1:]:
        load.start()

    barrier = pltpu.get_barrier_semaphore()
    pl.semaphore_signal(barrier, inc=1, device_id={"tensor": partner}, device_id_type=MESH)

    for step in range(fars - 1):
        pl.semaphore_signal(
            barrier, inc=1, device_id={"tensor": far_at(step) * 2 + near}, device_id_type=MESH
        )
    for hop in range(groups - 1):
        pl.semaphore_signal(
            barrier,
            inc=1,
            device_id={"dp": lax.rem(group + 1 + hop, groups)},
            device_id_type=MESH,
        )
    pl.semaphore_wait(barrier, fars + groups - 1)

    def remote(source, target, sems, index, device):
        return pltpu.make_async_remote_copy(
            src_ref=source,
            dst_ref=target,
            send_sem=sems.at[0, index],
            recv_sem=sems.at[1, index],
            device_id={"tensor": device},
            device_id_type=MESH,
        )

    map_copy = remote(conv_ref, map_recv, map_sems, 0, partner)
    map_copy.start()
    count_copies = []
    for hop in range(groups - 1):
        copy = pltpu.make_async_remote_copy(
            src_ref=count_ref,
            dst_ref=count_recv.at[hop],
            send_sem=count_sems.at[0, hop],
            recv_sem=count_sems.at[1, hop],
            device_id={"dp": lax.rem(group + 1 + hop, groups)},
            device_id_type=MESH,
        )
        copy.start()
        count_copies.append(copy)

    shape = (lanes, inner)
    target_head = iota(shape, 1) // head_dim
    lane_row = iota(shape, 0)
    for j in range(positions):
        place_buf[j] = (lane_row == target_head + j * heads).astype(F32).astype(BF16)
    to_heads = place_buf[0]

    lane_head = iota((1, inner), 1) // head_dim
    skip = jnp.zeros((1, inner), F32)
    for h in range(heads):
        skip = jnp.where(lane_head == h, skip_ref[h], skip)

    cache = cache_ref[...]
    kernel = kernel_ref[...].astype(F32)
    offset = offset_ref[...].astype(F32)

    def values_of(c):
        span = slice(c * height, (c + 1) * height)
        cached = spread_cache(cache, height, positions, c * per_chunk)
        return convolve(inner_ref[1, span].astype(F32), cached, kernel, offset, positions)

    def wait_maps():
        map_copy.wait_recv()
        mine = conv_ref[...].astype(F32)
        other = map_recv[...].astype(F32)
        even = near == 0
        input_map[...] = jnp.where(even, mine, other)
        output_map[...] = jnp.where(even, other, mine)

    def front(c):
        span = slice(c * height, (c + 1) * height)
        values = values_of(c)
        gate = silu(inner_ref[0, span].astype(F32))
        if c == 0:
            wait_maps()
        outputs = output_map[span].astype(BF16)
        inputs = input_map[span].astype(BF16)
        align = dot_nt(outputs, inputs)
        square = (height, height)
        same = iota(square, 0) // positions == iota(square, 1) // positions
        fold = (height, lanes)
        folded = (iota(fold, 0) % positions == iota(fold, 1) // heads).astype(F32).astype(BF16)
        mix = (mix_ref[span] * dot_split(jnp.where(same, align, 0.0), folded)).astype(BF16)
        values3 = values.reshape(per_chunk, positions, inner)
        head = skip * values
        for j in range(positions):
            spread = jnp.broadcast_to(values3[:, j : j + 1], values3.shape).reshape(height, inner)
            head = head + dot(mix, place_buf[j]) * spread
        state_loads[c].wait()
        carried = jnp.concatenate(
            [
                dot_nt(
                    output_map[r * positions : (r + 1) * positions].astype(BF16), state_buf[r]
                )
                for r in range(c * per_chunk, (c + 1) * per_chunk)
            ],
            axis=0,
        )
        head = head + carried * dot_split(after_ref[span], to_heads)
        gated = head * gate
        squares = jnp.sum(gated * gated, axis=1, keepdims=True)
        sq_send[c] = jnp.broadcast_to(squares, sq_send.shape[1:])
        sq_copies[c].start()
        weighted_buf[span] = values * dot_split(keep_ref[span], to_heads)
        return (gated * gain_ref[...]).astype(BF16)

    sq_copies = [
        remote(sq_send.at[c], sq_recv.at[c], sq_sems, c, partner) for c in range(chunks)
    ]
    y_copies = [remote(y_send.at[c], y_recv.at[c], y_sems, c, partner) for c in range(chunks)]
    z_copies = [
        [
            remote(
                z_send.at[c, step],
                z_recv.at[c, step],
                z_sems,
                c * (fars - 1) + step,
                far_at(step) * 2 + near,
            )
            for step in range(fars - 1)
        ]
        for c in range(chunks)
    ]

    def region(c, plane, owner):
        return out_buf.at[pl.ds(c * height, height), cols(plane * half + owner * width, width)]

    def owned(c, owner, sems, index, device, plane=near):
        return remote(region(c, plane, owner), region(c, plane, owner), sems, index, device)

    def send_partial(c):
        rows_in = front(c)
        if c == 0:
            weight_loads[0].wait()
        y_send[c] = dot(rows_in, weight_buf[0]).astype(BF16)
        y_copies[c].start()
        if c == 0:
            weight_loads[1].wait()
        acc_buf[c] = dot(rows_in, weight_buf[1])

    def pair_sum(c):
        span = slice(c * height, (c + 1) * height)
        sq_copies[c].wait_recv()
        total = (sq_send[c] + sq_recv[c])[:, :1] / (2 * inner)
        scale = lax.rsqrt(total + EPSILON) * valid_ref[span, :1]
        y_copies[c].wait_recv()
        acc_buf[c] = (acc_buf[c] + y_recv[c].astype(F32)) * scale

        for step in range(fars - 1):
            z_send[c, step] = acc_buf[c, :, cols(far_at(step) * width, width)].astype(BF16)
            z_copies[c][step].start()

    sent = []

    def send_final(c):
        total = acc_buf[c, :, cols(far * width, width)]
        for step in range(fars - 1):
            z_copies[c][step].wait_recv()
            total = total + z_recv[c, step].astype(F32)
        span = pl.ds(c * height, height)
        out_buf[span, cols(near * half + far * width, width)] = total.astype(BF16)
        copies = [owned(c, far, p_sems, c * fars, partner)]
        for step in range(fars - 1):
            index = c * (fars - 1) + step
            copies.append(owned(c, far, o_sems, index, far_at(step) * 2 + near))
        for copy in copies:
            copy.start()
            sent.append(copy)

    def forward(c):
        for step in range(fars - 1):
            index = c * (fars - 1) + step
            owned(c, far_of(step), o_sems, index, partner).wait_recv()
            copy = owned(c, far_of(step), p_sems, c * fars + 1 + step, partner)
            copy.start()
            sent.append(copy)

    def complete(c):
        owned(c, far, p_sems, c * fars, partner, 1 - near).wait_recv()
        for step in range(fars - 1):
            index = c * fars + 1 + step
            owned(c, far_of(step), p_sems, index, partner, 1 - near).wait_recv()

    def keep_state(c):
        for r in range(c * per_chunk, (c + 1) * per_chunk):
            span = slice(r * positions, (r + 1) * positions)
            added = dot_tn(weighted_buf[span].astype(BF16), input_map[span].astype(BF16))
            for h in range(heads):
                block = slice(h * head_dim, (h + 1) * head_dim)
                kept_buf[r, block] = (
                    scale_ref[r, h] * state_buf[r, block].astype(F32) + added[block]
                ).astype(BF16)

    stages = (
        (send_partial, 0),
        (pair_sum, 2),
        (send_final, 4),
        (forward, 6),
        (keep_state, 4),
        (complete, 9),
    )
    for slot in range(chunks + max(lag for _, lag in stages)):
        for stage, lag in stages:
            if 0 <= slot - lag < chunks:
                stage(slot - lag)

    count = count_ref[...]
    for hop in range(groups - 1):
        count_copies[hop].wait_recv()
        count = count + count_recv[hop]
    total_ref[0] = count[0, 0]

    for copy in [map_copy] + sq_copies + y_copies + sum(z_copies, []) + sent + count_copies:
        copy.wait_send()


def finish_kernel(
    rows_ref,
    kept_ref,
    inner_ref,
    cache_ref,
    fresh_pick_ref,
    cache_pick_ref,
    rows_hbm,
    kept_hbm,
    value_kept_hbm,
    value_kept_ref,
    sems,
):
    copies = [
        pltpu.make_async_copy(rows_ref, rows_hbm, sems.at[0]),
        pltpu.make_async_copy(kept_ref, kept_hbm, sems.at[1]),
        pltpu.make_async_copy(value_kept_ref, value_kept_hbm, sems.at[2]),
    ]
    copies[0].start()
    copies[1].start()
    depth, requests, inner = cache_ref.shape
    cache_rows = cache_ref[...].reshape(depth * requests, inner)
    value_kept = dot(fresh_pick_ref[...], inner_ref[1]) + dot(cache_pick_ref[...], cache_rows)
    value_kept_ref[...] = value_kept.reshape(value_kept_ref.shape).astype(BF16)
    copies[2].start()
    for copy in copies:
        copy.wait()


def local(
    tokens,
    norm_gain,
    in_weight,
    group_weight,
    step_weight,
    value_kernel,
    value_offset,
    group_kernel,
    group_offset,
    step_bias,
    decay_rate,
    skip_gain,
    out_gain,
    out_weight,
    scan_state,
    value_cache,
    group_cache,
    accepted,
    draft_lengths,
    live_flags,
):
    requests, positions, model_width = tokens.shape
    rows = requests * positions
    heads, head_dim, state_size = scan_state.shape[1:]
    inner = heads * head_dim
    map_width = group_weight.shape[1]
    depth = value_cache.shape[1]
    lanes = positions * heads
    groups = lax.axis_size("dp")
    chunks = next(c for c in (6, 4, 3, 2, 1) if requests % c == 0 and (rows // c) % 16 == 0)
    height = rows // chunks
    half = model_width // 2
    vmem = pl.BlockSpec(memory_space=pltpu.VMEM)
    smem = pl.BlockSpec(memory_space=pltpu.SMEM)
    hbm = pl.BlockSpec(memory_space=pltpu.HBM)

    def pinned(array):
        return pltpu.with_memory_space_constraint(array, pltpu.HBM)

    def shaped(dims, kind):
        return jax.ShapeDtypeStruct(dims, kind)

    (
        normed,
        conv,
        mix,
        keep,
        after,
        kept_scale,
        valid,
        fresh_pick,
        cache_pick,
        group_kept,
        own_total,
    ) = pl.pallas_call(
        prepare_kernel,
        out_shape=[
            shaped((rows, model_width), BF16),
            shaped((rows, map_width), BF16),
            shaped((rows, lanes), F32),
            shaped((rows, lanes), F32),
            shaped((rows, lanes), F32),
            shaped((requests, heads), F32),
            shaped((rows, 128), F32),
            shaped((depth * requests, rows), BF16),
            shaped((depth * requests, depth * requests), BF16),
            pltpu.HBM((depth, requests, map_width), BF16),
            shaped((8, 128), jnp.int32),
        ],
        in_specs=[hbm] * 12,
        out_specs=[vmem] * 9 + [hbm, vmem],
        scratch_shapes=[
            pltpu.SMEM((requests,), jnp.int32),
            pltpu.SMEM((requests,), jnp.int32),
            pltpu.SMEM((requests,), jnp.int32),
            pltpu.VMEM((rows, model_width), BF16),
            pltpu.VMEM((1, model_width), F32),
            pltpu.VMEM(group_weight.shape, BF16),
            pltpu.VMEM(step_weight.shape[::-1], BF16),
            pltpu.VMEM((depth, requests, map_width), BF16),
            pltpu.VMEM(group_kernel.shape, BF16),
            pltpu.VMEM((1, map_width), BF16),
            pltpu.VMEM((1, heads), F32),
            pltpu.VMEM((1, heads), F32),
            pltpu.VMEM((depth, requests, map_width), BF16),
            pltpu.SemaphoreType.DMA((12,)),
            pltpu.SemaphoreType.DMA,
        ],
        compiler_params=pltpu.CompilerParams(vmem_limit_bytes=32 * 1024 * 1024),
    )(
        pinned(accepted),
        pinned(draft_lengths),
        pinned(live_flags),
        pinned(tokens.reshape(rows, model_width)),
        pinned(norm_gain.reshape(1, -1)),
        pinned(group_weight),
        pinned(step_weight.T),
        pinned(jnp.transpose(group_cache, (1, 0, 2))),
        pinned(group_kernel),
        pinned(group_offset.reshape(1, -1)),
        pinned(step_bias.reshape(1, -1)),
        pinned(decay_rate.reshape(1, -1)),
    )
    normed, value_offset = lax.optimization_barrier((normed, value_offset))
    inner_proj = jnp.einsum(
        "rd,dgi->gri", normed, in_weight, preferred_element_type=F32
    ).astype(BF16)

    cache_rows = jnp.transpose(value_cache, (1, 0, 2))
    fars = lax.axis_size("tensor") // 2
    block = (chunks, fars - 1, height, half // fars)
    out_rows, kept_state, totals = pl.pallas_call(
        layer_kernel,
        out_shape=[
            shaped((rows, model_width), BF16),
            shaped((requests, inner, state_size), BF16),
            shaped((1,), jnp.int32),
        ],
        in_specs=[smem] * 2 + [vmem] * 11 + [hbm] * 2,
        out_specs=[vmem, vmem, smem],
        scratch_shapes=[
            pltpu.VMEM((2, inner, half), BF16),
            pltpu.VMEM((requests, inner, state_size), BF16),
            pltpu.VMEM((chunks, height, half), BF16),
            pltpu.VMEM((chunks, height, half), BF16),
            pltpu.VMEM(block, BF16),
            pltpu.VMEM(block, BF16),
            pltpu.VMEM((chunks, height, half), F32),
            pltpu.VMEM((positions, lanes, inner), BF16),
            pltpu.VMEM((rows, map_width), BF16),
            pltpu.VMEM((rows, map_width), F32),
            pltpu.VMEM((rows, map_width), F32),
            pltpu.VMEM((rows, inner), F32),
            pltpu.VMEM((chunks, height, 128), F32),
            pltpu.VMEM((chunks, height, 128), F32),
            pltpu.VMEM((groups - 1, 8, 128), jnp.int32),
            pltpu.SemaphoreType.DMA((2,)),
            pltpu.SemaphoreType.DMA((chunks,)),
            pltpu.SemaphoreType.DMA((2, 1)),
            pltpu.SemaphoreType.DMA((2, chunks)),
            pltpu.SemaphoreType.DMA((2, chunks)),
            pltpu.SemaphoreType.DMA((2, chunks * (fars - 1))),
            pltpu.SemaphoreType.DMA((2, chunks * (fars - 1))),
            pltpu.SemaphoreType.DMA((2, chunks * fars)),
            pltpu.SemaphoreType.DMA((2, groups - 1)),
        ],
        compiler_params=pltpu.CompilerParams(
            collective_id=0, has_side_effects=True, vmem_limit_bytes=40 * 1024 * 1024
        ),
    )(
        kept_scale,
        skip_gain,
        inner_proj,
        conv,
        mix,
        keep,
        after,
        valid,
        cache_rows,
        value_kernel,
        value_offset.reshape(1, -1),
        out_gain.reshape(1, -1),
        own_total,
        pinned(out_weight),
        pinned(scan_state.reshape(requests, inner, state_size)),
    )
    out_rows, kept_state, value_kept = pl.pallas_call(
        finish_kernel,
        out_shape=[
            pltpu.HBM((rows, model_width), BF16),
            pltpu.HBM((requests, inner, state_size), BF16),
            pltpu.HBM((depth, requests, inner), BF16),
        ],
        in_specs=[vmem] * 6,
        out_specs=[hbm] * 3,
        scratch_shapes=[
            pltpu.VMEM((depth, requests, inner), BF16),
            pltpu.SemaphoreType.DMA((3,)),
        ],
        compiler_params=pltpu.CompilerParams(vmem_limit_bytes=16 * 1024 * 1024),
    )(out_rows, kept_state, inner_proj, cache_rows, fresh_pick, cache_pick)
    return (
        out_rows.reshape(requests, positions, model_width),
        kept_state.reshape(scan_state.shape),
        jnp.transpose(value_kept, (1, 0, 2)),
        jnp.transpose(group_kept, (1, 0, 2)),
        totals,
    )


def solution(mesh):
    placed = (
        P("dp", None, None),
        P(),
        P(None, None, "tensor"),
        P(None, "tensor"),
        P(None, "tensor"),
        P(None, "tensor"),
        P("tensor"),
        P(None, "tensor"),
        P("tensor"),
        P("tensor"),
        P("tensor"),
        P("tensor"),
        P("tensor"),
        P("tensor", None),
        P("dp", "tensor", None, None),
        P("dp", None, "tensor"),
        P("dp", None, "tensor"),
        P("dp"),
        P("dp"),
        P("dp"),
    )
    return jax.shard_map(
        local,
        mesh=mesh,
        in_specs=placed,
        out_specs=(
            P("dp", None, None),
            P("dp", "tensor", None, None),
            P("dp", None, "tensor"),
            P("dp", None, "tensor"),
            P(),
        ),
        check_vma=False,
    )
```

time: 93 us -> 70.9 us (0.76)
  matrix products: 19.9 us -> 5.22 us
  Pallas kernels: 51.1 us -> 62.9 us
  other arithmetic: 9.74 us -> 0 us
  local copies, waits for them, and re-layouts: 7.55 us -> 0.04 us
  starting transfers between devices: 3.14 us -> 0 us
  between operations: 1.06 us -> 2.44 us
    dot_general x7 -> x1, matrix products: 19.9 us -> 5.22 us  [local(): jnp.einsum('rd,dgi->gri', normed, in_weight, preferred_element_type=F32)]
    pallas_call x1 -> x3, Pallas kernels: 51.1 us -> 62.9 us  [the longest x1 56.5 us: local(): pl.pallas_call(layer_kernel, out_shape=[shaped((rows, model_width), BF16)...]
    unnamed x46 -> x10, local copies, waits for them, and re-layouts: 3.61 us -> 0.03 us
    reduce_sum x4 -> x0, other arithmetic: 3.46 us -> none  [the longest x1 1.8 us: local(): jnp.mean(wide * wide, axis=2, keepdims=True) + EPSILON]
    ppermute x2 -> x0, starting transfers between devices: 3.14 us -> none  [swapped(): return lax.ppermute(value, axis, pairs)]
    convert_element_type x7 -> x0, other arithmetic: 2.84 us -> none  [the longest x2 1.12 us: narrow(): return value.astype(jnp.bfloat16)]
    exp x2 -> x0, local copies, waits for them, and re-layouts: 1.39 us -> none  [the longest x1 1.31 us: local(): jnp.exp(prefix_kept)[:, :, None, None] * initial]
    select_n x2 -> x0, other arithmetic: 1.26 us -> none  [keep_window(): jnp.where(chosen, sequence[:, start_row:start_row + width_rows], kept)]
  transfers between devices with their start and end apart: 2 -> 0, of which waited for: 0 -> 0; matrix products, arithmetic and copies ran while one was open for 23% -> 0% of each run, Pallas kernels for 0% -> 0%
where the time goes in v1:
time: 70.9 us; the launch traced here: 70.6 us
  Pallas kernels  62.9 us (89%)
  matrix products  5.22 us (7%)
  between operations  2.44 us (3%)
    pallas_call x1, Pallas kernels, local(): pl.pallas_call(layer_kernel, out_shape=[shaped((rows, model_width), BF16)...  56.5 us
    dot_general x1, matrix products, local(): jnp.einsum('rd,dgi->gri', normed, in_weight, preferred_element_type=F32)  5.22 us
    pallas_call x1, Pallas kernels, local(): pl.pallas_call(prepare_kernel, out_shape=[shaped((rows, model_width), BF1...  4.23 us
    pallas_call x1, Pallas kernels, local(): pl.pallas_call(finish_kernel, out_shape=[pltpu.HBM((rows, model_width), B...  2.23 us

profile of v1, /device:TPU:0, one launch (start us, length us, event | category | flops | bytes accessed | tf_op | source)
XLA Modules:
  0.0 70.6 jit_solution(4662054800897649319)
XLA Ops:
  0.6 4.2 %shard_map.227 = (bf16[192,4096]{1,0:T(8,128)(2,1)S(1)}, bf16[192,128]{1,0:T(8,128)(2,1)S(1)}, f32[192,64]{1,0:T(8,128)S(1)}, f32[192,64]{1,0:T(8,128)S(1)}, f32...) custom-call(s32[24]{0:T(128)} %accepted_hbm.1, ...), custom_call_target="tpu_custom_call" | custom-call | tf_op jit(solution)/shard_map/pallas_call | solution.py:611
  4.9 0.0 copy-start.4
  4.9 0.0 copy-start
  4.9 0.0 copy-start.1
  4.9 0.0 copy-start.2
  4.9 0.0 copy-start.3
  4.9 5.2 %fusion.8.inner_ref = bf16[2,192,512]{2,1,0:T(8,128)(2,1)S(1)} fusion(bf16[4096,2,512]{2,1,0:T(2,128)(2,1)} %param.22, bf16[192,4096]{1,0:T(8,128)(2,1)S(1)} %get-tuple-element.26), kind=kOutput, calls=%fused_computation.4 | convolution fusion | flops 1610809344 | bytes 10354688 | tf_op jit(solution)/shard_map/rd,dgi->gri/dot_general | solution.py:661
  10.2 0.0 copy-done.4
  10.2 0.0 copy-done
  10.2 0.0 copy-done.1
  10.2 0.0 copy-done.2
  10.2 0.0 copy-done.3
  10.2 56.5 %shard_map.228 = (bf16[192,4096]{1,0:T(8,128)(2,1)S(1)}, bf16[24,512,128]{2,1,0:T(8,128)(2,1)S(1)}, s32[1]{0:T(128)}) custom-call(f32[24,8]{1,0:T(8,128)S(1)} %get-tuple-element.24.scale_ref, f32[8]{0:T(128)S(1)} %copy-done.3, bf16[2,192,512]{2,1,0:T(8,128)(2,1)S(1)} %fusion.8.inner_ref, bf16[192,128]{1,0:T(8,128)(2,1)S(1)} %get-tuple-element.27.conv_ref, ...), custom_call_target="tpu_custom_call" | custom-call | tf_op jit(solution)/shard_map/pallas_call | solution.py:668
  66.7 2.2 %shard_map.229 = (bf16[192,4096]{1,0:T(8,128)(2,1)}, bf16[24,512,128]{2,1,0:T(8,128)(2,1)}, bf16[3,24,512]{2,1,0:T(8,128)(2,1)}) custom-call(bf16[192,4096]{1,0:T(8,128)(2,1)S(1)} %get-tuple-element.34.rows_ref, bf16[24,512,128]{2,1,0:T(8,128)(2,1)S(1)} %get-tuple-element.35.kept_ref, bf16[2,192,512]{2,1,0:T(8,128)(2,1)S(1)} %fusion.8.inner_ref, ...), custom_call_target="tpu_custom_call" | custom-call | tf_op jit(solution)/shard_map/pallas_call | solution.py:723
  (1 shorter events, 0.0 us)
Async XLA Ops:
  4.9 5.3 %copy-start.4 = (bf16[512]{0:T(512)(128)(2,1)S(1)}, bf16[512]{0:T(512)(128)(2,1)}, u32[]{:S(2)}) copy-start(bf16[512]{0:T(512)(128)(2,1)} %param.26) | copy-start | bytes 3076
  4.9 5.3 %copy-start = (bf16[24,3,512]{2,0,1:T(8,128)(2,1)S(1)}, bf16[24,3,512]{2,0,1:T(8,128)(2,1)}, u32[]{:S(2)}) copy-start(bf16[24,3,512]{2,0,1:T(8,128)(2,1)} %param.35) | copy-start | bytes 221188
  4.9 5.3 %copy-start.1 = (bf16[4,512]{1,0:T(4,128)(2,1)S(1)}, bf16[4,512]{1,0:T(4,128)(2,1)}, u32[]{:S(2)}) copy-start(bf16[4,512]{1,0:T(4,128)(2,1)} %kernel_ref.1) | copy-start | bytes 12292
  4.9 5.3 %copy-start.2 = (f32[512]{0:T(512)S(1)}, f32[512]{0:T(512)}, u32[]{:S(2)}) copy-start(f32[512]{0:T(512)} %param.32) | copy-start | bytes 6148
  4.9 5.3 %copy-start.3 = (f32[8]{0:T(128)S(1)}, f32[8]{0:T(128)}, u32[]{:S(2)}) copy-start(f32[8]{0:T(128)} %skip_ref.1) | copy-start | bytes 100

commit v2 on v1

--- a/solution.py
+++ b/solution.py
@@ -75,7 +75,9 @@
     bias_hbm,
     rate_hbm,
     normed_ref,
-    conv_ref,
+    input_map_ref,
+    output_map_ref,
+    group_proj_ref,
     mix_ref,
     keep_ref,
     after_ref,
@@ -83,7 +85,6 @@
     valid_ref,
     fresh_pick_ref,
     cache_pick_ref,
-    group_kept_hbm,
     total_ref,
     accepted_ref,
     draft_ref,
@@ -97,10 +98,16 @@
     offset_ref,
     bias_ref,
     rate_ref,
-    group_kept_ref,
+    map_send,
+    map_recv,
     load_sems,
-    kept_sem,
+    map_sems,
 ):
+    me = lax.axis_index("tensor")
+    near = me % 2
+    partner = me + 1 - 2 * near
+    barrier = pltpu.get_barrier_semaphore()
+    pl.semaphore_signal(barrier, inc=1, device_id={"tensor": partner}, device_id_type=MESH)
     sources = (gain_hbm, tokens_hbm, weight_hbm, step_weight_hbm, cache_hbm)
     sources += (kernel_hbm, offset_hbm, bias_hbm, rate_hbm, accepted_hbm, draft_hbm, live_hbm)
     targets = (gain_ref, tokens_ref, weight_ref, step_weight_ref, cache_ref)
@@ -130,7 +137,7 @@
         load.wait()
     normed = normed_ref[...]
     group_proj = dot(normed, weight_ref[...]).astype(BF16)
-    step_raw = dot_nt(normed, step_weight_ref[...])
+    group_proj_ref[...] = group_proj
 
     cache = cache_ref[...]
     cached = spread_cache(cache, rows, positions, 0)
@@ -141,7 +148,18 @@
         offset_ref[...].astype(F32),
         positions,
     )
-    conv_ref[...] = conv.astype(BF16)
+    map_send[...] = conv.astype(BF16)
+    pl.semaphore_wait(barrier, 1)
+    map_copy = pltpu.make_async_remote_copy(
+        src_ref=map_send,
+        dst_ref=map_recv,
+        send_sem=map_sems.at[0],
+        recv_sem=map_sems.at[1],
+        device_id={"tensor": partner},
+        device_id_type=MESH,
+    )
+    map_copy.start()
+    step_raw = dot_nt(normed, step_weight_ref[...])
 
     counts = [accepted_ref[r] * live_ref[r] for r in range(requests)]
     total = counts[0]
@@ -205,18 +223,19 @@
     cache_pick = picks(depth * requests, lambda col: col // requests, lambda col: col % requests)
     fresh_pick_ref[...] = fresh_pick
     cache_pick_ref[...] = cache_pick
-    kept_rows = dot(fresh_pick, group_proj) + dot(cache_pick, cache.reshape(depth * requests, -1))
-    group_kept_ref[...] = kept_rows.reshape(group_kept_ref.shape).astype(BF16)
-    kept_copy = pltpu.make_async_copy(group_kept_ref, group_kept_hbm, kept_sem)
-    kept_copy.start()
-    kept_copy.wait()
+    map_copy.wait_recv()
+    mine, other = map_send[...].astype(F32), map_recv[...].astype(F32)
+    input_map_ref[...] = jnp.where(near == 0, mine, other).astype(BF16)
+    output_map_ref[...] = jnp.where(near == 0, other, mine).astype(BF16)
+    map_copy.wait_send()
 
 
 def layer_kernel(
     scale_ref,
     skip_ref,
     inner_ref,
-    conv_ref,
+    input_map,
+    output_map,
     mix_ref,
     keep_ref,
     after_ref,
@@ -235,23 +254,22 @@
     state_buf,
     y_send,
     y_recv,
-    z_send,
-    z_recv,
+    n_send,
+    n_recv,
+    f_send,
+    f_recv,
     acc_buf,
     place_buf,
-    map_recv,
-    input_map,
-    output_map,
     weighted_buf,
     sq_send,
     sq_recv,
     count_recv,
     weight_sem,
     state_sem,
-    map_sems,
     sq_sems,
     y_sems,
-    z_sems,
+    n_sems,
+    f_sems,
     o_sems,
     p_sems,
     count_sems,
@@ -273,11 +291,21 @@
     far, near = me // 2, me % 2
     partner = far * 2 + (1 - near)
 
-    def far_at(step):
-        return lax.rem(far + 1 + step, fars)
-
-    def far_of(step):
-        return lax.rem(far - 1 - step + 2 * fars, fars)
+    team = fars // 2
+    wing, seat = far // team, far % team
+    mate = (1 - wing) * team + seat
+
+    def peer_at(step):
+        return wing * team + lax.rem(seat + 1 + step, team)
+
+    def peer_of(step):
+        return wing * team + lax.rem(seat - 1 - step + 2 * team, team)
+
+    def across(place):
+        return lax.rem(place + team, fars)
+
+    def device(place):
+        return place * 2 + near
 
     groups = lax.axis_size("dp")
     group = lax.axis_index("dp")
@@ -310,9 +338,9 @@
     barrier = pltpu.get_barrier_semaphore()
     pl.semaphore_signal(barrier, inc=1, device_id={"tensor": partner}, device_id_type=MESH)
 
-    for step in range(fars - 1):
+    for place in [mate] + [peer_at(step) for step in range(team - 1)]:
         pl.semaphore_signal(
-            barrier, inc=1, device_id={"tensor": far_at(step) * 2 + near}, device_id_type=MESH
+            barrier, inc=1, device_id={"tensor": device(place)}, device_id_type=MESH
         )
     for hop in range(groups - 1):
         pl.semaphore_signal(
@@ -321,8 +349,6 @@
             device_id={"dp": lax.rem(group + 1 + hop, groups)},
             device_id_type=MESH,
         )
-    pl.semaphore_wait(barrier, fars + groups - 1)
-
     def remote(source, target, sems, index, device):
         return pltpu.make_async_remote_copy(
             src_ref=source,
@@ -333,21 +359,6 @@
             device_id_type=MESH,
         )
 
-    map_copy = remote(conv_ref, map_recv, map_sems, 0, partner)
-    map_copy.start()
-    count_copies = []
-    for hop in range(groups - 1):
-        copy = pltpu.make_async_remote_copy(
-            src_ref=count_ref,
-            dst_ref=count_recv.at[hop],
-            send_sem=count_sems.at[0, hop],
-            recv_sem=count_sems.at[1, hop],
-            device_id={"dp": lax.rem(group + 1 + hop, groups)},
-            device_id_type=MESH,
-        )
-        copy.start()
-        count_copies.append(copy)
-
     shape = (lanes, inner)
     target_head = iota(shape, 1) // head_dim
     lane_row = iota(shape, 0)
@@ -369,23 +380,11 @@
         cached = spread_cache(cache, height, positions, c * per_chunk)
         return convolve(inner_ref[1, span].astype(F32), cached, kernel, offset, positions)
 
-    def wait_maps():
-        map_copy.wait_recv()
-        mine = conv_ref[...].astype(F32)
-        other = map_recv[...].astype(F32)
-        even = near == 0
-        input_map[...] = jnp.where(even, mine, other)
-        output_map[...] = jnp.where(even, other, mine)
-
     def front(c):
         span = slice(c * height, (c + 1) * height)
         values = values_of(c)
         gate = silu(inner_ref[0, span].astype(F32))
-        if c == 0:
-            wait_maps()
-        outputs = output_map[span].astype(BF16)
-        inputs = input_map[span].astype(BF16)
-        align = dot_nt(outputs, inputs)
+        align = dot_nt(output_map[span], input_map[span])
         square = (height, height)
         same = iota(square, 0) // positions == iota(square, 1) // positions
         fold = (height, lanes)
@@ -397,10 +396,11 @@
             spread = jnp.broadcast_to(values3[:, j : j + 1], values3.shape).reshape(height, inner)
             head = head + dot(mix, place_buf[j]) * spread
         state_loads[c].wait()
+        outputs = output_map[span].astype(F32)
         carried = jnp.concatenate(
             [
                 dot_nt(
-                    output_map[r * positions : (r + 1) * positions].astype(BF16), state_buf[r]
+                    outputs[(r - c * per_chunk) * positions :][:positions].astype(BF16), state_buf[r]
                 )
                 for r in range(c * per_chunk, (c + 1) * per_chunk)
             ],
@@ -410,6 +410,8 @@
         gated = head * gate
         squares = jnp.sum(gated * gated, axis=1, keepdims=True)
         sq_send[c] = jnp.broadcast_to(squares, sq_send.shape[1:])
+        if c == 0:
+            pl.semaphore_wait(barrier, fars // 2 + groups)
         sq_copies[c].start()
         weighted_buf[span] = values * dot_split(keep_ref[span], to_heads)
         return (gated * gain_ref[...]).astype(BF16)
@@ -418,18 +420,21 @@
         remote(sq_send.at[c], sq_recv.at[c], sq_sems, c, partner) for c in range(chunks)
     ]
     y_copies = [remote(y_send.at[c], y_recv.at[c], y_sems, c, partner) for c in range(chunks)]
-    z_copies = [
+    n_copies = [
         [
             remote(
-                z_send.at[c, step],
-                z_recv.at[c, step],
-                z_sems,
-                c * (fars - 1) + step,
-                far_at(step) * 2 + near,
+                n_send.at[c, step],
+                n_recv.at[c, step],
+                n_sems,
+                c * (team - 1) + step,
+                device(peer_at(step)),
             )
-            for step in range(fars - 1)
+            for step in range(team - 1)
         ]
         for c in range(chunks)
+    ]
+    f_copies = [
+        remote(f_send.at[c], f_recv.at[c], f_sems, c, device(mate)) for c in range(chunks)
     ]
 
     def region(c, plane, owner):
@@ -456,63 +461,104 @@
         y_copies[c].wait_recv()
         acc_buf[c] = (acc_buf[c] + y_recv[c].astype(F32)) * scale
 
-        for step in range(fars - 1):
-            z_send[c, step] = acc_buf[c, :, cols(far_at(step) * width, width)].astype(BF16)
-            z_copies[c][step].start()
+        for step in range(team - 1):
+            place = peer_at(step)
+            n_send[c, step, 0] = acc_buf[c, :, cols(place * width, width)].astype(BF16)
+            n_send[c, step, 1] = acc_buf[c, :, cols(across(place) * width, width)].astype(BF16)
+            n_copies[c][step].start()
+
+    def team_sum(c):
+        own = acc_buf[c, :, cols(far * width, width)]
+        other = acc_buf[c, :, cols(mate * width, width)]
+        for step in range(team - 1):
+            n_copies[c][step].wait_recv()
+            own = own + n_recv[c, step, 0].astype(F32)
+            other = other + n_recv[c, step, 1].astype(F32)
+        f_send[c] = other.astype(BF16)
+        f_copies[c].start()
+        acc_buf[c, :, cols(far * width, width)] = own
 
     sent = []
 
+    def send(copy):
+        copy.start()
+        sent.append(copy)
+
+    per_o, per_p = 2 * team - 1, 2 * team
+
     def send_final(c):
-        total = acc_buf[c, :, cols(far * width, width)]
-        for step in range(fars - 1):
-            z_copies[c][step].wait_recv()
-            total = total + z_recv[c, step].astype(F32)
+        f_copies[c].wait_recv()
+        total = acc_buf[c, :, cols(far * width, width)] + f_recv[c].astype(F32)
         span = pl.ds(c * height, height)
         out_buf[span, cols(near * half + far * width, width)] = total.astype(BF16)
-        copies = [owned(c, far, p_sems, c * fars, partner)]
-        for step in range(fars - 1):
-            index = c * (fars - 1) + step
-            copies.append(owned(c, far, o_sems, index, far_at(step) * 2 + near))
-        for copy in copies:
-            copy.start()
-            sent.append(copy)
+        send(owned(c, far, o_sems, c * per_o, device(mate)))
+        for step in range(team - 1):
+            send(owned(c, far, o_sems, c * per_o + 1 + step, device(peer_at(step))))
+        send(owned(c, far, p_sems, c * per_p, partner))
 
     def forward(c):
-        for step in range(fars - 1):
-            index = c * (fars - 1) + step
-            owned(c, far_of(step), o_sems, index, partner).wait_recv()
-            copy = owned(c, far_of(step), p_sems, c * fars + 1 + step, partner)
-            copy.start()
-            sent.append(copy)
+        owned(c, mate, o_sems, c * per_o, partner).wait_recv()
+        for step in range(team - 1):
+            send(owned(c, mate, o_sems, c * per_o + team + step, device(peer_at(step))))
+        send(owned(c, mate, p_sems, c * per_p + 1, partner))
+        for step in range(team - 1):
+            place = peer_of(step)
+            owned(c, place, o_sems, c * per_o + 1 + step, partner).wait_recv()
+            send(owned(c, place, p_sems, c * per_p + 2 + step, partner))
+
+    def forward_last(c):
+        for step in range(team - 1):
+            place = across(peer_of(step))
+            owned(c, place, o_sems, c * per_o + team + step, partner).wait_recv()
+            send(owned(c, place, p_sems, c * per_p + team + 1 + step, partner))
 
     def complete(c):
-        owned(c, far, p_sems, c * fars, partner, 1 - near).wait_recv()
-        for step in range(fars - 1):
-            index = c * fars + 1 + step
-            owned(c, far_of(step), p_sems, index, partner, 1 - near).wait_recv()
+        places = [far, mate]
+        places += [peer_of(step) for step in range(team - 1)]
+        places += [across(peer_of(step)) for step in range(team - 1)]
+        for index, place in enumerate(places):
+            owned(c, place, p_sems, c * per_p + index, partner, 1 - near).wait_recv()
 
     def keep_state(c):
         for r in range(c * per_chunk, (c + 1) * per_chunk):
             span = slice(r * positions, (r + 1) * positions)
-            added = dot_tn(weighted_buf[span].astype(BF16), input_map[span].astype(BF16))
+            added = dot_tn(weighted_buf[span].astype(BF16), input_map[span])
             for h in range(heads):
                 block = slice(h * head_dim, (h + 1) * head_dim)
                 kept_buf[r, block] = (
                     scale_ref[r, h] * state_buf[r, block].astype(F32) + added[block]
                 ).astype(BF16)
 
-    stages = (
-        (send_partial, 0),
-        (pair_sum, 2),
-        (send_final, 4),
-        (forward, 6),
-        (keep_state, 4),
-        (complete, 9),
-    )
-    for slot in range(chunks + max(lag for _, lag in stages)):
-        for stage, lag in stages:
-            if 0 <= slot - lag < chunks:
-                stage(slot - lag)
+    plan = (
+        (send_partial, 0, 2.8),
+        (pair_sum, 5.1, 2.8),
+        (team_sum, 8.8, 2.8),
+        (send_final, 11.8, 2.8),
+        (forward, 14.8, 2.8),
+        (forward_last, 17.8, 2.8),
+        (keep_state, 18, 1.4),
+        (complete, 40.0, 1.0),
+    )
+    events = [
+        (first + spacing * c, index, c)
+        for index, (_, first, spacing) in enumerate(plan)
+        for c in range(chunks)
+    ]
+    count_copies = []
+    for _, index, c in sorted(events):
+        plan[index][0](c)
+        if plan[index][0] is send_partial and c == 0:
+            for hop in range(groups - 1):
+                copy = pltpu.make_async_remote_copy(
+                    src_ref=count_ref,
+                    dst_ref=count_recv.at[hop],
+                    send_sem=count_sems.at[0, hop],
+                    recv_sem=count_sems.at[1, hop],
+                    device_id={"dp": lax.rem(group + 1 + hop, groups)},
+                    device_id_type=MESH,
+                )
+                copy.start()
+                count_copies.append(copy)
 
     count = count_ref[...]
     for hop in range(groups - 1):
@@ -520,7 +566,7 @@
         count = count + count_recv[hop]
     total_ref[0] = count[0, 0]
 
-    for copy in [map_copy] + sq_copies + y_copies + sum(z_copies, []) + sent + count_copies:
+    for copy in sq_copies + y_copies + sum(n_copies, []) + f_copies + sent + count_copies:
         copy.wait_send()
 
 
@@ -529,26 +575,34 @@
     kept_ref,
     inner_ref,
     cache_ref,
+    group_proj_ref,
+    group_cache_ref,
     fresh_pick_ref,
     cache_pick_ref,
     rows_hbm,
     kept_hbm,
     value_kept_hbm,
+    group_kept_hbm,
     value_kept_ref,
+    group_kept_ref,
     sems,
 ):
     copies = [
         pltpu.make_async_copy(rows_ref, rows_hbm, sems.at[0]),
         pltpu.make_async_copy(kept_ref, kept_hbm, sems.at[1]),
         pltpu.make_async_copy(value_kept_ref, value_kept_hbm, sems.at[2]),
+        pltpu.make_async_copy(group_kept_ref, group_kept_hbm, sems.at[3]),
     ]
     copies[0].start()
     copies[1].start()
-    depth, requests, inner = cache_ref.shape
-    cache_rows = cache_ref[...].reshape(depth * requests, inner)
-    value_kept = dot(fresh_pick_ref[...], inner_ref[1]) + dot(cache_pick_ref[...], cache_rows)
-    value_kept_ref[...] = value_kept.reshape(value_kept_ref.shape).astype(BF16)
-    copies[2].start()
+    def kept(fresh, cache, target, copy):
+        flat = cache.reshape(-1, cache.shape[2])
+        rows = dot(fresh_pick_ref[...], fresh) + dot(cache_pick_ref[...], flat)
+        target[...] = rows.reshape(target.shape).astype(BF16)
+        copy.start()
+
+    kept(inner_ref[1], cache_ref[...], value_kept_ref, copies[2])
+    kept(group_proj_ref[...], group_cache_ref[...], group_kept_ref, copies[3])
     for copy in copies:
         copy.wait()
 
@@ -598,7 +652,9 @@
 
     (
         normed,
-        conv,
+        input_map,
+        output_map,
+        group_proj,
         mix,
         keep,
         after,
@@ -606,12 +662,13 @@
         valid,
         fresh_pick,
         cache_pick,
-        group_kept,
         own_total,
     ) = pl.pallas_call(
         prepare_kernel,
         out_shape=[
             shaped((rows, model_width), BF16),
+            shaped((rows, map_width), BF16),
+            shaped((rows, map_width), BF16),
             shaped((rows, map_width), BF16),
             shaped((rows, lanes), F32),
             shaped((rows, lanes), F32),
@@ -620,11 +677,10 @@
             shaped((rows, 128), F32),
             shaped((depth * requests, rows), BF16),
             shaped((depth * requests, depth * requests), BF16),
-            pltpu.HBM((depth, requests, map_width), BF16),
             shaped((8, 128), jnp.int32),
         ],
         in_specs=[hbm] * 12,
-        out_specs=[vmem] * 9 + [hbm, vmem],
+        out_specs=[vmem] * 12,
         scratch_shapes=[
             pltpu.SMEM((requests,), jnp.int32),
             pltpu.SMEM((requests,), jnp.int32),
@@ -638,11 +694,14 @@
             pltpu.VMEM((1, map_width), BF16),
             pltpu.VMEM((1, heads), F32),
             pltpu.VMEM((1, heads), F32),
-            pltpu.VMEM((depth, requests, map_width), BF16),
+            pltpu.VMEM((rows, map_width), BF16),
+            pltpu.VMEM((rows, map_width), BF16),
             pltpu.SemaphoreType.DMA((12,)),
-            pltpu.SemaphoreType.DMA,
+            pltpu.SemaphoreType.DMA((2,)),
         ],
-        compiler_params=pltpu.CompilerParams(vmem_limit_bytes=32 * 1024 * 1024),
+        compiler_params=pltpu.CompilerParams(
+            collective_id=1, has_side_effects=True, vmem_limit_bytes=32 * 1024 * 1024
+        ),
     )(
         pinned(accepted),
         pinned(draft_lengths),
@@ -664,7 +723,8 @@
 
     cache_rows = jnp.transpose(value_cache, (1, 0, 2))
     fars = lax.axis_size("tensor") // 2
-    block = (chunks, fars - 1, height, half // fars)
+    team = fars // 2
+    width = half // fars
     out_rows, kept_state, totals = pl.pallas_call(
         layer_kernel,
         out_shape=[
@@ -672,32 +732,31 @@
             shaped((requests, inner, state_size), BF16),
             shaped((1,), jnp.int32),
         ],
-        in_specs=[smem] * 2 + [vmem] * 11 + [hbm] * 2,
+        in_specs=[smem] * 2 + [vmem] * 12 + [hbm] * 2,
         out_specs=[vmem, vmem, smem],
         scratch_shapes=[
             pltpu.VMEM((2, inner, half), BF16),
             pltpu.VMEM((requests, inner, state_size), BF16),
             pltpu.VMEM((chunks, height, half), BF16),
             pltpu.VMEM((chunks, height, half), BF16),
-            pltpu.VMEM(block, BF16),
-            pltpu.VMEM(block, BF16),
+            pltpu.VMEM((chunks, team - 1, 2, height, width), BF16),
+            pltpu.VMEM((chunks, team - 1, 2, height, width), BF16),
+            pltpu.VMEM((chunks, height, width), BF16),
+            pltpu.VMEM((chunks, height, width), BF16),
             pltpu.VMEM((chunks, height, half), F32),
             pltpu.VMEM((positions, lanes, inner), BF16),
-            pltpu.VMEM((rows, map_width), BF16),
-            pltpu.VMEM((rows, map_width), F32),
-            pltpu.VMEM((rows, map_width), F32),
             pltpu.VMEM((rows, inner), F32),
             pltpu.VMEM((chunks, height, 128), F32),
             pltpu.VMEM((chunks, height, 128), F32),
             pltpu.VMEM((groups - 1, 8, 128), jnp.int32),
             pltpu.SemaphoreType.DMA((2,)),
             pltpu.SemaphoreType.DMA((chunks,)),
-            pltpu.SemaphoreType.DMA((2, 1)),
             pltpu.SemaphoreType.DMA((2, chunks)),
             pltpu.SemaphoreType.DMA((2, chunks)),
-            pltpu.SemaphoreType.DMA((2, chunks * (fars - 1))),
-            pltpu.SemaphoreType.DMA((2, chunks * (fars - 1))),
-            pltpu.SemaphoreType.DMA((2, chunks * fars)),
+            pltpu.SemaphoreType.DMA((2, chunks * (team - 1))),
+            pltpu.SemaphoreType.DMA((2, chunks)),
+            pltpu.SemaphoreType.DMA((2, chunks * (2 * team - 1))),
+            pltpu.SemaphoreType.DMA((2, chunks * 2 * team)),
             pltpu.SemaphoreType.DMA((2, groups - 1)),
         ],
         compiler_params=pltpu.CompilerParams(
@@ -707,7 +766,8 @@
         kept_scale,
         skip_gain,
         inner_proj,
-        conv,
+        input_map,
+        output_map,
         mix,
         keep,
         after,
@@ -720,21 +780,33 @@
         pinned(out_weight),
         pinned(scan_state.reshape(requests, inner, state_size)),
     )
-    out_rows, kept_state, value_kept = pl.pallas_call(
+    group_rows = jnp.transpose(group_cache, (1, 0, 2))
+    out_rows, kept_state, value_kept, group_kept = pl.pallas_call(
         finish_kernel,
         out_shape=[
             pltpu.HBM((rows, model_width), BF16),
             pltpu.HBM((requests, inner, state_size), BF16),
             pltpu.HBM((depth, requests, inner), BF16),
+            pltpu.HBM((depth, requests, map_width), BF16),
         ],
-        in_specs=[vmem] * 6,
-        out_specs=[hbm] * 3,
+        in_specs=[vmem] * 8,
+        out_specs=[hbm] * 4,
         scratch_shapes=[
             pltpu.VMEM((depth, requests, inner), BF16),
-            pltpu.SemaphoreType.DMA((3,)),
+            pltpu.VMEM((depth, requests, map_width), BF16),
+            pltpu.SemaphoreType.DMA((4,)),
         ],
         compiler_params=pltpu.CompilerParams(vmem_limit_bytes=16 * 1024 * 1024),
-    )(out_rows, kept_state, inner_proj, cache_rows, fresh_pick, cache_pick)
+    )(
+        out_rows,
+        kept_state,
+        inner_proj,
+        cache_rows,
+        group_proj,
+        group_rows,
+        fresh_pick,
+        cache_pick,
+    )
     return (
         out_rows.reshape(requests, positions, model_width),
         kept_state.reshape(scan_state.shape),

time: 70.9 us -> 66.5 us (0.938)
  Pallas kernels: 62.9 us -> 58.4 us
    pallas_call x1, Pallas kernels: 56.5 us -> 47.7 us  [local(): pl.pallas_call(layer_kernel, out_shape=[shaped((rows, model_width), BF16)...]
    pallas_call x1, Pallas kernels: 4.23 us -> 8.47 us  [local(): pl.pallas_call(prepare_kernel, out_shape=[shaped((rows, model_width), BF1...]
where the time goes in v2:
time: 66.5 us; the launch traced here: 66.2 us
  Pallas kernels  58.4 us (88%)
  matrix products  5.21 us (8%)
  between operations  2.57 us (4%)
    pallas_call x1, Pallas kernels, local(): pl.pallas_call(layer_kernel, out_shape=[shaped((rows, model_width), BF16)...  47.7 us
    pallas_call x1, Pallas kernels, local(): pl.pallas_call(prepare_kernel, out_shape=[shaped((rows, model_width), BF1...  8.47 us
    dot_general x1, matrix products, local(): jnp.einsum('rd,dgi->gri', normed, in_weight, preferred_element_type=F32)  5.21 us
    pallas_call x1, Pallas kernels, local(): pl.pallas_call(finish_kernel, out_shape=[pltpu.HBM((rows, model_width), B...  2.23 us

profile of v2, /device:TPU:0, one launch (start us, length us, event | category | flops | bytes accessed | tf_op | source)
XLA Modules:
  0.0 66.2 jit_solution(9090392399110695721)
XLA Ops:
  0.6 8.5 %shard_map.227 = (bf16[192,4096]{1,0:T(8,128)(2,1)S(1)}, bf16[192,128]{1,0:T(8,128)(2,1)S(1)}, bf16[192,128]{1,0:T(8,128)(2,1)S(1)}, bf16[192,128]{1,0:T(8,128)(...) custom-call(s32[24]{0:T(128)} %accepted_hbm.1, ...), custom_call_target="tpu_custom_call" | custom-call | tf_op jit(solution)/shard_map/pallas_call | solution.py:666
  9.1 0.0 copy-start.5
  9.1 0.0 copy-start
  9.1 0.0 copy-start.2
  9.1 0.0 copy-start.3
  9.2 0.0 copy-start.4
  9.2 5.2 %fusion.8.inner_ref = bf16[2,192,512]{2,1,0:T(8,128)(2,1)S(1)} fusion(bf16[4096,2,512]{2,1,0:T(2,128)(2,1)} %param.22, bf16[192,4096]{1,0:T(8,128)(2,1)S(1)} %get-tuple-element.28), kind=kOutput, calls=%fused_computation.4 | convolution fusion | flops 1610809344 | bytes 10354688 | tf_op jit(solution)/shard_map/rd,dgi->gri/dot_general | solution.py:720
  14.4 0.0 copy-done.5
  14.4 0.0 copy-done
  14.4 0.0 copy-done.2
  14.4 0.0 copy-done.3
  14.4 0.0 copy-done.4
  14.5 0.0 copy-start.1
  14.5 47.7 %shard_map.228 = (bf16[192,4096]{1,0:T(8,128)(2,1)S(1)}, bf16[24,512,128]{2,1,0:T(8,128)(2,1)S(1)}, s32[1]{0:T(128)}) custom-call(f32[24,8]{1,0:T(8,128)S(1)} %get-tuple-element.26.scale_ref, f32[8]{0:T(128)S(1)} %copy-done.4, bf16[2,192,512]{2,1,0:T(8,128)(2,1)S(1)} %fusion.8.inner_ref, bf16[192,128]{1,0:T(8,128)(2,1)S(1)} %get-tuple-element.29.input_map, ...), custom_call_target="tpu_custom_call" | custom-call | tf_op jit(solution)/shard_map/pallas_call | solution.py:728
  62.1 0.0 copy-done.1
  62.2 2.2 %shard_map.229 = (bf16[192,4096]{1,0:T(8,128)(2,1)}, bf16[24,512,128]{2,1,0:T(8,128)(2,1)}, bf16[3,24,512]{2,1,0:T(8,128)(2,1)}, bf16[3,24,128]{2,1,0:T(8,128)(2,1)}) custom-call(bf16[192,4096]{1,0:T(8,128)(2,1)S(1)} %get-tuple-element.37.rows_ref, bf16[24,512,128]{2,1,0:T(8,128)(2,1)S(1)} %get-tuple-element.38.kept_ref, ...), custom_call_target="tpu_custom_call" | custom-call | tf_op jit(solution)/shard_map/pallas_call | solution.py:784
  (1 shorter events, 0.0 us)
Async XLA Ops:
  9.1 5.3 %copy-start.5 = (bf16[512]{0:T(512)(128)(2,1)S(1)}, bf16[512]{0:T(512)(128)(2,1)}, u32[]{:S(2)}) copy-start(bf16[512]{0:T(512)(128)(2,1)} %param.26) | copy-start | bytes 3076
  9.1 5.3 %copy-start = (bf16[24,3,512]{2,0,1:T(8,128)(2,1)S(1)}, bf16[24,3,512]{2,0,1:T(8,128)(2,1)}, u32[]{:S(2)}) copy-start(bf16[24,3,512]{2,0,1:T(8,128)(2,1)} %param.35) | copy-start | bytes 221188
  9.1 5.3 %copy-start.2 = (bf16[4,512]{1,0:T(4,128)(2,1)S(1)}, bf16[4,512]{1,0:T(4,128)(2,1)}, u32[]{:S(2)}) copy-start(bf16[4,512]{1,0:T(4,128)(2,1)} %kernel_ref.1) | copy-start | bytes 12292
  9.1 5.3 %copy-start.3 = (f32[512]{0:T(512)S(1)}, f32[512]{0:T(512)}, u32[]{:S(2)}) copy-start(f32[512]{0:T(512)} %param.32) | copy-start | bytes 6148
  9.2 5.3 %copy-start.4 = (f32[8]{0:T(128)S(1)}, f32[8]{0:T(128)}, u32[]{:S(2)}) copy-start(f32[8]{0:T(128)} %skip_ref.1) | copy-start | bytes 100
  14.5 47.7 %copy-start.1 = (bf16[24,3,128]{2,0,1:T(8,128)(2,1)S(1)}, bf16[24,3,128]{2,0,1:T(8,128)(2,1)}, u32[]{:S(2)}) copy-start(bf16[24,3,128]{2,0,1:T(8,128)(2,1)} %param.36) | copy-start | bytes 55300

commit v3 on v2

--- a/solution.py
+++ b/solution.py
@@ -74,6 +74,8 @@
     offset_hbm,
     bias_hbm,
     rate_hbm,
+    in_weight_hbm,
+    out_weight_hbm,
     normed_ref,
     input_map_ref,
     output_map_ref,
@@ -86,6 +88,8 @@
     fresh_pick_ref,
     cache_pick_ref,
     total_ref,
+    in_weight_ref,
+    out_weight_ref,
     accepted_ref,
     draft_ref,
     live_ref,
@@ -102,6 +106,7 @@
     map_recv,
     load_sems,
     map_sems,
+    weight_sem,
 ):
     me = lax.axis_index("tensor")
     near = me % 2
@@ -127,6 +132,12 @@
     step = 16 if rows % 16 == 0 else 8
     loads[0].wait()
     loads[1].wait()
+    weight_loads = [
+        pltpu.make_async_copy(in_weight_hbm, in_weight_ref, weight_sem.at[0]),
+        pltpu.make_async_copy(out_weight_hbm, out_weight_ref, weight_sem.at[1]),
+    ]
+    for load in weight_loads:
+        load.start()
     for start in range(0, rows, step):
         wide = tokens_ref[start : start + step].astype(F32)
         mean = jnp.sum(wide * wide, axis=1, keepdims=True) / model_width
@@ -228,6 +239,12 @@
     input_map_ref[...] = jnp.where(near == 0, mine, other).astype(BF16)
     output_map_ref[...] = jnp.where(near == 0, other, mine).astype(BF16)
     map_copy.wait_send()
+    for load in weight_loads:
+        load.wait()
+
+
+def across_first_chunks(chunks):
+    return {1: 0} if chunks >= 6 else {}
 
 
 def layer_kernel(
@@ -245,12 +262,11 @@
     offset_ref,
     gain_ref,
     count_ref,
-    weight_hbm,
+    weight_ref,
     state_hbm,
     out_buf,
     kept_buf,
     total_ref,
-    weight_buf,
     state_buf,
     y_send,
     y_recv,
@@ -259,12 +275,16 @@
     f_send,
     f_recv,
     acc_buf,
+    zn_send,
+    zn_recv,
+    zf_send,
+    zf_recv,
+    zacc_buf,
     place_buf,
     weighted_buf,
     sq_send,
     sq_recv,
     count_recv,
-    weight_sem,
     state_sem,
     sq_sems,
     y_sems,
@@ -282,6 +302,7 @@
     heads = lanes // positions
     head_dim = inner // heads
     per_chunk = requests // chunks
+    across_first = across_first_chunks(chunks)
     depth = cache_ref.shape[0]
 
     members = lax.axis_size("tensor")
@@ -313,14 +334,6 @@
     def cols(start, width):
         return pl.ds(pl.multiple_of(start, width), width)
 
-    weight_loads = [
-        pltpu.make_async_copy(
-            weight_hbm.at[:, cols(block * half, half)],
-            weight_buf.at[slot],
-            weight_sem.at[slot],
-        )
-        for slot, block in enumerate((1 - near, near))
-    ]
     state_loads = [
         pltpu.make_async_copy(
             state_hbm.at[pl.ds(c * per_chunk, per_chunk)],
@@ -330,8 +343,6 @@
         for c in range(chunks)
     ]
     state_loads[0].start()
-    weight_loads[0].start()
-    weight_loads[1].start()
     for load in state_loads[1:]:
         load.start()
 
@@ -419,12 +430,17 @@
     sq_copies = [
         remote(sq_send.at[c], sq_recv.at[c], sq_sems, c, partner) for c in range(chunks)
     ]
-    y_copies = [remote(y_send.at[c], y_recv.at[c], y_sems, c, partner) for c in range(chunks)]
+    y_copies = [
+        remote(zf_send.at[across_first[c]], zf_recv.at[across_first[c]], y_sems, c, device(mate))
+        if c in across_first
+        else remote(y_send.at[c], y_recv.at[c], y_sems, c, partner)
+        for c in range(chunks)
+    ]
     n_copies = [
         [
             remote(
-                n_send.at[c, step],
-                n_recv.at[c, step],
+                zn_send.at[across_first[c], step] if c in across_first else n_send.at[c, step],
+                zn_recv.at[across_first[c], step] if c in across_first else n_recv.at[c, step],
                 n_sems,
                 c * (team - 1) + step,
                 device(peer_at(step)),
@@ -434,7 +450,14 @@
         for c in range(chunks)
     ]
     f_copies = [
-        remote(f_send.at[c], f_recv.at[c], f_sems, c, device(mate)) for c in range(chunks)
+        remote(
+            f_send.at[c],
+            f_recv.at[c],
+            f_sems,
+            c,
+            partner if c in across_first else device(mate),
+        )
+        for c in range(chunks)
     ]
 
     def region(c, plane, owner):
@@ -445,19 +468,58 @@
 
     def send_partial(c):
         rows_in = front(c)
-        if c == 0:
-            weight_loads[0].wait()
-        y_send[c] = dot(rows_in, weight_buf[0]).astype(BF16)
+        if c in across_first:
+            zacc_buf[across_first[c], 1] = dot(rows_in, weight_ref[:, cols((1 - near) * half, half)])
+            zacc_buf[across_first[c], 0] = dot(rows_in, weight_ref[:, cols(near * half, half)])
+            return
+        y_send[c] = dot(rows_in, weight_ref[:, cols((1 - near) * half, half)]).astype(BF16)
         y_copies[c].start()
-        if c == 0:
-            weight_loads[1].wait()
-        acc_buf[c] = dot(rows_in, weight_buf[1])
-
-    def pair_sum(c):
+        acc_buf[c] = dot(rows_in, weight_ref[:, cols(near * half, half)])
+
+    def row_scale(c):
         span = slice(c * height, (c + 1) * height)
         sq_copies[c].wait_recv()
         total = (sq_send[c] + sq_recv[c])[:, :1] / (2 * inner)
-        scale = lax.rsqrt(total + EPSILON) * valid_ref[span, :1]
+        return lax.rsqrt(total + EPSILON) * valid_ref[span, :1]
+
+    def across_scale(c):
+        k = across_first[c]
+        scale = row_scale(c)
+        for plane in range(2):
+            zacc_buf[k, plane] = zacc_buf[k, plane] * scale
+        for step in range(team - 1):
+            place = peer_at(step)
+            for plane in range(2):
+                for slot, owner in enumerate((place, across(place))):
+                    block = zacc_buf[k, plane, :, cols(owner * width, width)]
+                    zn_send[k, step, plane, slot] = block.astype(BF16)
+            n_copies[c][step].start()
+
+    def across_team(c):
+        k = across_first[c]
+        for plane in range(2):
+            own = zacc_buf[k, plane, :, cols(far * width, width)]
+            other = zacc_buf[k, plane, :, cols(mate * width, width)]
+            for step in range(team - 1):
+                if plane == 0:
+                    n_copies[c][step].wait_recv()
+                own = own + zn_recv[k, step, plane, 0].astype(F32)
+                other = other + zn_recv[k, step, plane, 1].astype(F32)
+            zf_send[k, plane] = other.astype(BF16)
+            zacc_buf[k, plane, :, cols(far * width, width)] = own
+        y_copies[c].start()
+
+    def across_pair(c):
+        k = across_first[c]
+        y_copies[c].wait_recv()
+        own = zacc_buf[k, 0, :, cols(far * width, width)] + zf_recv[k, 0].astype(F32)
+        other = zacc_buf[k, 1, :, cols(far * width, width)] + zf_recv[k, 1].astype(F32)
+        f_send[c] = other.astype(BF16)
+        f_copies[c].start()
+        acc_buf[c, :, cols(far * width, width)] = own
+
+    def pair_sum(c):
+        scale = row_scale(c)
         y_copies[c].wait_recv()
         acc_buf[c] = (acc_buf[c] + y_recv[c].astype(F32)) * scale
 
@@ -529,25 +591,36 @@
                     scale_ref[r, h] * state_buf[r, block].astype(F32) + added[block]
                 ).astype(BF16)
 
-    plan = (
-        (send_partial, 0, 2.8),
-        (pair_sum, 5.1, 2.8),
-        (team_sum, 8.8, 2.8),
-        (send_final, 11.8, 2.8),
-        (forward, 14.8, 2.8),
-        (forward_last, 17.8, 2.8),
-        (keep_state, 18, 1.4),
-        (complete, 40.0, 1.0),
-    )
-    events = [
-        (first + spacing * c, index, c)
-        for index, (_, first, spacing) in enumerate(plan)
-        for c in range(chunks)
-    ]
+    hop, wire = 2.7, 0.7 * height / 32
+    events = []
+    ready = 4 * wire
+    for c in range(chunks):
+        begin = 2.0 * c
+        events.append((begin, c, send_partial))
+        if c in across_first:
+            kind = across_first[c]
+            scaled = begin + 4.0
+            teamed = scaled + 4 * wire * (1 + kind) + hop
+            paired = teamed + 2 * wire + hop
+            summed = paired + wire + hop
+            events += [(scaled, c, across_scale), (teamed, c, across_team)]
+            events.append((paired, c, across_pair))
+        else:
+            paired = max(begin + 4 * wire, ready) + hop
+            ready = ready + 4 * wire
+            teamed = paired + 2 * wire + hop
+            summed = teamed + wire + hop
+            events += [(paired, c, pair_sum), (teamed, c, team_sum)]
+        events.append((summed, c, send_final))
+        events.append((summed + wire + hop, c, forward))
+        events.append((summed + 2 * (wire + hop), c, forward_last))
+        events.append((16.0 + 1.4 * c, c, keep_state))
+        events.append((100.0 + c, c, complete))
+    events.sort(key=lambda event: event[:2])
     count_copies = []
-    for _, index, c in sorted(events):
-        plan[index][0](c)
-        if plan[index][0] is send_partial and c == 0:
+    for _, c, stage in events:
+        stage(c)
+        if stage is send_partial and c == 0:
             for hop in range(groups - 1):
                 copy = pltpu.make_async_remote_copy(
                     src_ref=count_ref,
@@ -663,6 +736,8 @@
         fresh_pick,
         cache_pick,
         own_total,
+        in_weight,
+        out_weight,
     ) = pl.pallas_call(
         prepare_kernel,
         out_shape=[
@@ -678,9 +753,11 @@
             shaped((depth * requests, rows), BF16),
             shaped((depth * requests, depth * requests), BF16),
             shaped((8, 128), jnp.int32),
+            shaped(in_weight.shape, BF16),
+            shaped(out_weight.shape, BF16),
         ],
-        in_specs=[hbm] * 12,
-        out_specs=[vmem] * 12,
+        in_specs=[hbm] * 14,
+        out_specs=[vmem] * 14,
         scratch_shapes=[
             pltpu.SMEM((requests,), jnp.int32),
             pltpu.SMEM((requests,), jnp.int32),
@@ -698,9 +775,10 @@
             pltpu.VMEM((rows, map_width), BF16),
             pltpu.SemaphoreType.DMA((12,)),
             pltpu.SemaphoreType.DMA((2,)),
+            pltpu.SemaphoreType.DMA((2,)),
         ],
         compiler_params=pltpu.CompilerParams(
-            collective_id=1, has_side_effects=True, vmem_limit_bytes=32 * 1024 * 1024
+            collective_id=1, has_side_effects=True, vmem_limit_bytes=20 * 1024 * 1024
         ),
     )(
         pinned(accepted),
@@ -715,6 +793,8 @@
         pinned(group_offset.reshape(1, -1)),
         pinned(step_bias.reshape(1, -1)),
         pinned(decay_rate.reshape(1, -1)),
+        pinned(in_weight),
+        pinned(out_weight),
     )
     normed, value_offset = lax.optimization_barrier((normed, value_offset))
     inner_proj = jnp.einsum(
@@ -725,6 +805,7 @@
     fars = lax.axis_size("tensor") // 2
     team = fars // 2
     width = half // fars
+    kinds = max(1, len(across_first_chunks(chunks)))
     out_rows, kept_state, totals = pl.pallas_call(
         layer_kernel,
         out_shape=[
@@ -732,10 +813,9 @@
             shaped((requests, inner, state_size), BF16),
             shaped((1,), jnp.int32),
         ],
-        in_specs=[smem] * 2 + [vmem] * 12 + [hbm] * 2,
+        in_specs=[smem] * 2 + [vmem] * 13 + [hbm],
         out_specs=[vmem, vmem, smem],
         scratch_shapes=[
-            pltpu.VMEM((2, inner, half), BF16),
             pltpu.VMEM((requests, inner, state_size), BF16),
             pltpu.VMEM((chunks, height, half), BF16),
             pltpu.VMEM((chunks, height, half), BF16),
@@ -744,12 +824,16 @@
             pltpu.VMEM((chunks, height, width), BF16),
             pltpu.VMEM((chunks, height, width), BF16),
             pltpu.VMEM((chunks, height, half), F32),
+            pltpu.VMEM((kinds, team - 1, 2, 2, height, width), BF16),
+            pltpu.VMEM((kinds, team - 1, 2, 2, height, width), BF16),
+            pltpu.VMEM((kinds, 2, height, width), BF16),
+            pltpu.VMEM((kinds, 2, height, width), BF16),
+            pltpu.VMEM((kinds, 2, height, half), F32),
             pltpu.VMEM((positions, lanes, inner), BF16),
             pltpu.VMEM((rows, inner), F32),
             pltpu.VMEM((chunks, height, 128), F32),
             pltpu.VMEM((chunks, height, 128), F32),
             pltpu.VMEM((groups - 1, 8, 128), jnp.int32),
-            pltpu.SemaphoreType.DMA((2,)),
             pltpu.SemaphoreType.DMA((chunks,)),
             pltpu.SemaphoreType.DMA((2, chunks)),
             pltpu.SemaphoreType.DMA((2, chunks)),
@@ -760,7 +844,7 @@
             pltpu.SemaphoreType.DMA((2, groups - 1)),
         ],
         compiler_params=pltpu.CompilerParams(
-            collective_id=0, has_side_effects=True, vmem_limit_bytes=40 * 1024 * 1024
+            collective_id=0, has_side_effects=True, vmem_limit_bytes=32 * 1024 * 1024
         ),
     )(
         kept_scale,
@@ -777,7 +861,7 @@
         value_offset.reshape(1, -1),
         out_gain.reshape(1, -1),
         own_total,
-        pinned(out_weight),
+        out_weight,
         pinned(scan_state.reshape(requests, inner, state_size)),
     )
     group_rows = jnp.transpose(group_cache, (1, 0, 2))

time: 66.5 us -> 60.8 us (0.914)
  matrix products: 5.21 us -> 1.8 us
  Pallas kernels: 58.4 us -> 56.2 us
    dot_general x1, matrix products: 5.21 us -> 1.8 us  [local(): jnp.einsum('rd,dgi->gri', normed, in_weight, preferred_element_type=F32)]
    pallas_call x1, Pallas kernels: 47.7 us -> 45.5 us  [local(): pl.pallas_call(layer_kernel, out_shape=[shaped((rows, model_width), BF16)...]
where the time goes in v3:
time: 60.8 us; the launch traced here: 60.6 us
  Pallas kernels  56.2 us (92%)
  between operations  2.57 us (4%)
  matrix products  1.8 us (3%)
    pallas_call x1, Pallas kernels, local(): pl.pallas_call(layer_kernel, out_shape=[shaped((rows, model_width), BF16)...  45.5 us
    pallas_call x1, Pallas kernels, local(): pl.pallas_call(prepare_kernel, out_shape=[shaped((rows, model_width), BF1...  8.49 us
    pallas_call x1, Pallas kernels, local(): pl.pallas_call(finish_kernel, out_shape=[pltpu.HBM((rows, model_width), B...  2.23 us
    dot_general x1, matrix products, local(): jnp.einsum('rd,dgi->gri', normed, in_weight, preferred_element_type=F32)  1.8 us

profile of v3, /device:TPU:0, one launch (start us, length us, event | category | flops | bytes accessed | tf_op | source)
XLA Modules:
  0.0 60.6 jit_solution(12031659176046999934)
XLA Ops:
  0.6 8.5 %shard_map.227 = (bf16[192,4096]{1,0:T(8,128)(2,1)S(1)}, bf16[192,128]{1,0:T(8,128)(2,1)S(1)}, bf16[192,128]{1,0:T(8,128)(2,1)S(1)}, bf16[192,128]{1,0:T(8,128)(...) custom-call(s32[24]{0:T(128)} %accepted_hbm.1, ...), custom_call_target="tpu_custom_call" | custom-call | tf_op jit(solution)/shard_map/pallas_call | solution.py:741
  9.1 0.0 copy-start.5
  9.1 0.0 copy-start
  9.2 0.0 copy-start.2
  9.2 0.0 copy-start.3
  9.2 0.0 copy-start.4
  9.2 1.8 %fusion.8.inner_ref = bf16[2,192,512]{2,1,0:T(8,128)(2,1)S(1)} fusion(bf16[4096,2,512]{2,1,0:T(2,128)(2,1)S(1)} %get-tuple-element.29, bf16[192,4096]{1,0:T(8,128)(2,1)S(1)} %get-tuple-element.31), kind=kOutput, calls=%fused_computation.4 | convolution fusion | flops 1610809344 | bytes 10354688 | tf_op jit(solution)/shard_map/rd,dgi->gri/dot_general | solution.py:800
  11.0 0.0 copy-done.5
  11.0 0.0 copy-done
  11.0 0.0 copy-done.2
  11.0 0.0 copy-done.3
  11.0 0.0 copy-done.4
  11.1 0.0 copy-start.1
  11.1 45.5 %shard_map.228 = (bf16[192,4096]{1,0:T(8,128)(2,1)S(1)}, bf16[24,512,128]{2,1,0:T(8,128)(2,1)S(1)}, s32[1]{0:T(128)}) custom-call(f32[24,8]{1,0:T(8,128)S(1)} %get-tuple-element.28.scale_ref, f32[8]{0:T(128)S(1)} %copy-done.4, bf16[2,192,512]{2,1,0:T(8,128)(2,1)S(1)} %fusion.8.inner_ref, bf16[192,128]{1,0:T(8,128)(2,1)S(1)} %get-tuple-element.32.input_map, ...), custom_call_target="tpu_custom_call" | custom-call | tf_op jit(solution)/shard_map/pallas_call | solution.py:809
  56.5 0.0 copy-done.1
  56.5 2.2 %shard_map.229 = (bf16[192,4096]{1,0:T(8,128)(2,1)}, bf16[24,512,128]{2,1,0:T(8,128)(2,1)}, bf16[3,24,512]{2,1,0:T(8,128)(2,1)}, bf16[3,24,128]{2,1,0:T(8,128)(2,1)}) custom-call(bf16[192,4096]{1,0:T(8,128)(2,1)S(1)} %get-tuple-element.41.rows_ref, bf16[24,512,128]{2,1,0:T(8,128)(2,1)S(1)} %get-tuple-element.42.kept_ref, ...), custom_call_target="tpu_custom_call" | custom-call | tf_op jit(solution)/shard_map/pallas_call | solution.py:868
  (1 shorter events, 0.0 us)
Async XLA Ops:
  9.1 1.9 %copy-start.5 = (bf16[512]{0:T(512)(128)(2,1)S(1)}, bf16[512]{0:T(512)(128)(2,1)}, u32[]{:S(2)}) copy-start(bf16[512]{0:T(512)(128)(2,1)} %param.26) | copy-start | bytes 3076
  9.1 1.9 %copy-start = (bf16[24,3,512]{2,0,1:T(8,128)(2,1)S(1)}, bf16[24,3,512]{2,0,1:T(8,128)(2,1)}, u32[]{:S(2)}) copy-start(bf16[24,3,512]{2,0,1:T(8,128)(2,1)} %param.35) | copy-start | bytes 221188
  9.2 1.9 %copy-start.2 = (bf16[4,512]{1,0:T(4,128)(2,1)S(1)}, bf16[4,512]{1,0:T(4,128)(2,1)}, u32[]{:S(2)}) copy-start(bf16[4,512]{1,0:T(4,128)(2,1)} %kernel_ref.1) | copy-start | bytes 12292
  9.2 1.9 %copy-start.3 = (f32[512]{0:T(512)S(1)}, f32[512]{0:T(512)}, u32[]{:S(2)}) copy-start(f32[512]{0:T(512)} %param.32) | copy-start | bytes 6148
  9.2 1.9 %copy-start.4 = (f32[8]{0:T(128)S(1)}, f32[8]{0:T(128)}, u32[]{:S(2)}) copy-start(f32[8]{0:T(128)} %skip_ref.1) | copy-start | bytes 100
  11.1 45.5 %copy-start.1 = (bf16[24,3,128]{2,0,1:T(8,128)(2,1)S(1)}, bf16[24,3,128]{2,0,1:T(8,128)(2,1)}, u32[]{:S(2)}) copy-start(bf16[24,3,128]{2,0,1:T(8,128)(2,1)} %param.36) | copy-start | bytes 55300

commit v4 on v3

--- a/solution.py
+++ b/solution.py
@@ -75,7 +75,6 @@
     bias_hbm,
     rate_hbm,
     in_weight_hbm,
-    out_weight_hbm,
     normed_ref,
     input_map_ref,
     output_map_ref,
@@ -89,7 +88,6 @@
     cache_pick_ref,
     total_ref,
     in_weight_ref,
-    out_weight_ref,
     accepted_ref,
     draft_ref,
     live_ref,
@@ -134,7 +132,6 @@
     loads[1].wait()
     weight_loads = [
         pltpu.make_async_copy(in_weight_hbm, in_weight_ref, weight_sem.at[0]),
-        pltpu.make_async_copy(out_weight_hbm, out_weight_ref, weight_sem.at[1]),
     ]
     for load in weight_loads:
         load.start()
@@ -303,6 +300,7 @@
     head_dim = inner // heads
     per_chunk = requests // chunks
     across_first = across_first_chunks(chunks)
+    direct = set(range(chunks - 2, chunks))
     depth = cache_ref.shape[0]
 
     members = lax.axis_size("tensor")
@@ -349,7 +347,9 @@
     barrier = pltpu.get_barrier_semaphore()
     pl.semaphore_signal(barrier, inc=1, device_id={"tensor": partner}, device_id_type=MESH)
 
-    for place in [mate] + [peer_at(step) for step in range(team - 1)]:
+    others = [mate] + [peer_at(step) for step in range(team - 1)]
+    others += [across(peer_at(step)) for step in range(team - 1)]
+    for place in others:
         pl.semaphore_signal(
             barrier, inc=1, device_id={"tensor": device(place)}, device_id_type=MESH
         )
@@ -422,7 +422,7 @@
         squares = jnp.sum(gated * gated, axis=1, keepdims=True)
         sq_send[c] = jnp.broadcast_to(squares, sq_send.shape[1:])
         if c == 0:
-            pl.semaphore_wait(barrier, fars // 2 + groups)
+            pl.semaphore_wait(barrier, fars + groups - 1)
         sq_copies[c].start()
         weighted_buf[span] = values * dot_split(keep_ref[span], to_heads)
         return (gated * gain_ref[...]).astype(BF16)
@@ -556,11 +556,15 @@
         send(owned(c, far, o_sems, c * per_o, device(mate)))
         for step in range(team - 1):
             send(owned(c, far, o_sems, c * per_o + 1 + step, device(peer_at(step))))
+        if c in direct:
+            for step in range(team - 1):
+                target = device(across(peer_at(step)))
+                send(owned(c, far, o_sems, c * per_o + team + step, target))
         send(owned(c, far, p_sems, c * per_p, partner))
 
     def forward(c):
         owned(c, mate, o_sems, c * per_o, partner).wait_recv()
-        for step in range(team - 1):
+        for step in range(team - 1 if c not in direct else 0):
             send(owned(c, mate, o_sems, c * per_o + team + step, device(peer_at(step))))
         send(owned(c, mate, p_sems, c * per_p + 1, partner))
         for step in range(team - 1):
@@ -591,7 +595,7 @@
                     scale_ref[r, h] * state_buf[r, block].astype(F32) + added[block]
                 ).astype(BF16)
 
-    hop, wire = 2.7, 0.7 * height / 32
+    hop, wire = 2.2, 0.7 * height / 32
     events = []
     ready = 4 * wire
     for c in range(chunks):
@@ -613,7 +617,8 @@
             events += [(paired, c, pair_sum), (teamed, c, team_sum)]
         events.append((summed, c, send_final))
         events.append((summed + wire + hop, c, forward))
-        events.append((summed + 2 * (wire + hop), c, forward_last))
+        last = summed + 3 * wire + hop + 0.8 if c in direct else summed + 2 * (wire + hop)
+        events.append((last, c, forward_last))
         events.append((16.0 + 1.4 * c, c, keep_state))
         events.append((100.0 + c, c, complete))
     events.sort(key=lambda event: event[:2])
@@ -661,21 +666,25 @@
     sems,
 ):
     copies = [
-        pltpu.make_async_copy(rows_ref, rows_hbm, sems.at[0]),
-        pltpu.make_async_copy(kept_ref, kept_hbm, sems.at[1]),
-        pltpu.make_async_copy(value_kept_ref, value_kept_hbm, sems.at[2]),
-        pltpu.make_async_copy(group_kept_ref, group_kept_hbm, sems.at[3]),
+        pltpu.make_async_copy(value_kept_ref, value_kept_hbm, sems.at[0]),
+        pltpu.make_async_copy(group_kept_ref, group_kept_hbm, sems.at[1]),
     ]
-    copies[0].start()
-    copies[1].start()
+    cuts = 4 if kept_ref.shape[0] % 4 == 0 and rows_ref.shape[0] % 64 == 0 else 1
+    for source, target, base in ((kept_ref, kept_hbm, 2), (rows_ref, rows_hbm, 2 + cuts)):
+        size = source.shape[0] // cuts
+        for cut in range(cuts):
+            span = pl.ds(cut * size, size)
+            copy = pltpu.make_async_copy(source.at[span], target.at[span], sems.at[base + cut])
+            copy.start()
+            copies.append(copy)
     def kept(fresh, cache, target, copy):
         flat = cache.reshape(-1, cache.shape[2])
         rows = dot(fresh_pick_ref[...], fresh) + dot(cache_pick_ref[...], flat)
         target[...] = rows.reshape(target.shape).astype(BF16)
         copy.start()
 
-    kept(inner_ref[1], cache_ref[...], value_kept_ref, copies[2])
-    kept(group_proj_ref[...], group_cache_ref[...], group_kept_ref, copies[3])
+    kept(inner_ref[1], cache_ref[...], value_kept_ref, copies[0])
+    kept(group_proj_ref[...], group_cache_ref[...], group_kept_ref, copies[1])
     for copy in copies:
         copy.wait()
 
@@ -737,7 +746,6 @@
         cache_pick,
         own_total,
         in_weight,
-        out_weight,
     ) = pl.pallas_call(
         prepare_kernel,
         out_shape=[
@@ -754,10 +762,9 @@
             shaped((depth * requests, depth * requests), BF16),
             shaped((8, 128), jnp.int32),
             shaped(in_weight.shape, BF16),
-            shaped(out_weight.shape, BF16),
         ],
-        in_specs=[hbm] * 14,
-        out_specs=[vmem] * 14,
+        in_specs=[hbm] * 13,
+        out_specs=[vmem] * 13,
         scratch_shapes=[
             pltpu.SMEM((requests,), jnp.int32),
             pltpu.SMEM((requests,), jnp.int32),
@@ -794,7 +801,6 @@
         pinned(step_bias.reshape(1, -1)),
         pinned(decay_rate.reshape(1, -1)),
         pinned(in_weight),
-        pinned(out_weight),
     )
     normed, value_offset = lax.optimization_barrier((normed, value_offset))
     inner_proj = jnp.einsum(
@@ -878,7 +884,7 @@
         scratch_shapes=[
             pltpu.VMEM((depth, requests, inner), BF16),
             pltpu.VMEM((depth, requests, map_width), BF16),
-            pltpu.SemaphoreType.DMA((4,)),
+            pltpu.SemaphoreType.DMA((10,)),
         ],
         compiler_params=pltpu.CompilerParams(vmem_limit_bytes=16 * 1024 * 1024),
     )(

time: 60.8 us -> 60 us (0.987)
  Pallas kernels: 56.2 us -> 55.1 us
    pallas_call x1, Pallas kernels: 45.5 us -> 44.3 us  [local(): pl.pallas_call(layer_kernel, out_shape=[shaped((rows, model_width), BF16)...]
where the time goes in v4:
time: 60 us; the launch traced here: 59.8 us
  Pallas kernels  55.1 us (92%)
  between operations  2.5 us (4%)
  matrix products  1.79 us (3%)
    pallas_call x1, Pallas kernels, local(): pl.pallas_call(layer_kernel, out_shape=[shaped((rows, model_width), BF16)...  44.3 us
    pallas_call x1, Pallas kernels, local(): pl.pallas_call(prepare_kernel, out_shape=[shaped((rows, model_width), BF1...  8.49 us
    pallas_call x1, Pallas kernels, local(): pl.pallas_call(finish_kernel, out_shape=[pltpu.HBM((rows, model_width), B...  2.29 us
    dot_general x1, matrix products, local(): jnp.einsum('rd,dgi->gri', normed, in_weight, preferred_element_type=F32)  1.79 us

profile of v4, /device:TPU:0, one launch (start us, length us, event | category | flops | bytes accessed | tf_op | source)
XLA Modules:
  0.0 59.8 jit_solution(9444776592774399133)
XLA Ops:
  0.6 8.5 %shard_map.227 = (bf16[192,4096]{1,0:T(8,128)(2,1)S(1)}, bf16[192,128]{1,0:T(8,128)(2,1)S(1)}, bf16[192,128]{1,0:T(8,128)(2,1)S(1)}, bf16[192,128]{1,0:T(8,128)(...) custom-call(s32[24]{0:T(128)} %accepted_hbm.1, ...), custom_call_target="tpu_custom_call" | custom-call | tf_op jit(solution)/shard_map/pallas_call | solution.py:749
  9.1 0.0 copy-start.6
  9.1 0.0 copy-start
  9.2 0.0 copy-start.1
  9.2 0.0 copy-start.3
  9.2 0.0 copy-start.4
  9.2 0.0 copy-start.5
  9.2 1.8 %fusion.8.inner_ref = bf16[2,192,512]{2,1,0:T(8,128)(2,1)S(1)} fusion(bf16[4096,2,512]{2,1,0:T(2,128)(2,1)S(1)} %get-tuple-element.28, bf16[192,4096]{1,0:T(8,128)(2,1)S(1)} %get-tuple-element.30), kind=kOutput, calls=%fused_computation.4 | convolution fusion | flops 1610809344 | bytes 10354688 | tf_op jit(solution)/shard_map/rd,dgi->gri/dot_general | solution.py:806
  11.0 0.0 copy-done.6
  11.0 0.3 copy-done
  11.3 0.0 copy-done.1
  11.3 0.0 copy-done.3
  11.3 0.0 copy-done.4
  11.3 0.0 copy-done.5
  11.3 0.0 copy-start.2
  11.4 44.3 %shard_map.228 = (bf16[192,4096]{1,0:T(8,128)(2,1)S(1)}, bf16[24,512,128]{2,1,0:T(8,128)(2,1)S(1)}, s32[1]{0:T(128)}) custom-call(f32[24,8]{1,0:T(8,128)S(1)} %get-tuple-element.27.scale_ref, f32[8]{0:T(128)S(1)} %copy-done.5, bf16[2,192,512]{2,1,0:T(8,128)(2,1)S(1)} %fusion.8.inner_ref, bf16[192,128]{1,0:T(8,128)(2,1)S(1)} %get-tuple-element.31.input_map, ...), custom_call_target="tpu_custom_call" | custom-call | tf_op jit(solution)/shard_map/pallas_call | solution.py:815
  55.7 0.0 copy-done.2
  55.7 2.3 %shard_map.229 = (bf16[192,4096]{1,0:T(8,128)(2,1)}, bf16[24,512,128]{2,1,0:T(8,128)(2,1)}, bf16[3,24,512]{2,1,0:T(8,128)(2,1)}, bf16[3,24,128]{2,1,0:T(8,128)(2,1)}) custom-call(bf16[192,4096]{1,0:T(8,128)(2,1)S(1)} %get-tuple-element.39.rows_ref, bf16[24,512,128]{2,1,0:T(8,128)(2,1)S(1)} %get-tuple-element.40.kept_ref, ...), custom_call_target="tpu_custom_call" | custom-call | tf_op jit(solution)/shard_map/pallas_call | solution.py:874
  (1 shorter events, 0.0 us)
Async XLA Ops:
  9.1 1.9 %copy-start.6 = (bf16[512]{0:T(512)(128)(2,1)S(1)}, bf16[512]{0:T(512)(128)(2,1)}, u32[]{:S(2)}) copy-start(bf16[512]{0:T(512)(128)(2,1)} %param.26) | copy-start | bytes 3076
  9.1 2.2 %copy-start = (bf16[512,4096]{1,0:T(8,128)(2,1)S(1)}, bf16[512,4096]{1,0:T(8,128)(2,1)}, u32[]{:S(2)}) copy-start(bf16[512,4096]{1,0:T(8,128)(2,1)} %weight_ref.1) | copy-start | bytes 12582916
  9.2 2.2 %copy-start.1 = (bf16[24,3,512]{2,0,1:T(8,128)(2,1)S(1)}, bf16[24,3,512]{2,0,1:T(8,128)(2,1)}, u32[]{:S(2)}) copy-start(bf16[24,3,512]{2,0,1:T(8,128)(2,1)} %param.35) | copy-start | bytes 221188
  9.2 2.2 %copy-start.3 = (bf16[4,512]{1,0:T(4,128)(2,1)S(1)}, bf16[4,512]{1,0:T(4,128)(2,1)}, u32[]{:S(2)}) copy-start(bf16[4,512]{1,0:T(4,128)(2,1)} %kernel_ref.1) | copy-start | bytes 12292
  9.2 2.2 %copy-start.4 = (f32[512]{0:T(512)S(1)}, f32[512]{0:T(512)}, u32[]{:S(2)}) copy-start(f32[512]{0:T(512)} %param.32) | copy-start | bytes 6148
  9.2 2.2 %copy-start.5 = (f32[8]{0:T(128)S(1)}, f32[8]{0:T(128)}, u32[]{:S(2)}) copy-start(f32[8]{0:T(128)} %skip_ref.1) | copy-start | bytes 100
  11.3 44.3 %copy-start.2 = (bf16[24,3,128]{2,0,1:T(8,128)(2,1)S(1)}, bf16[24,3,128]{2,0,1:T(8,128)(2,1)}, u32[]{:S(2)}) copy-start(bf16[24,3,128]{2,0,1:T(8,128)(2,1)} %param.36) | copy-start | bytes 55300
